TPU v7x, 64 devices: a 2x2x8 block of a 4x4x8 slice. The times are simulated.
64 devices in a mesh: dp: 4 (over x, y), pp: 16 (over z, core).
Axes of the slice: x: 2, y: 2, z: 8, core: 2. Of those that a mesh axis runs over, the one named last changes fastest.
The devices are a block of a 4x4x8 slice.
Arguments:
- hidden: bfloat16 [128, 512, 576], P(('dp', 'pp')), parts along dimension 0
- labels: int32 [128, 512], P(('dp', 'pp')), parts along dimension 0
- gamma: float32 [576], replicated
- table: bfloat16 [49152, 576], P('pp')
Outputs:
- output 1: float32 [128, 512], P(('dp', 'pp')), parts along dimension 0
- output 2: bfloat16 [128, 512, 576], P(('dp', 'pp')), parts along dimension 0
- output 3: float32 [4], P('dp'), parts along dimension 0
- output 4: float32 [196608, 576], P(('dp', 'pp')), parts along dimension 0
- output 5: float32 [2304], P('dp'), parts along dimension 0
There are 4 independent parts. A program takes and returns all parts, laid end to end along the dimension named above; an argument that names none is the same for every part.
All inputs are finite; a program needn't handle non-finite values.
Results may differ from a plain program's by a relative error of at most 0.001.
Values are sent between devices in bfloat16 or wider.
A program may use at most 768 MiB of HBM per device.

v0:
```python
import jax
import jax.numpy as jnp
from jax import lax
from jax.sharding import PartitionSpec as P

SOFT_CAP = 30.0
EPS = 1e-6


def norm_rows(rows, gain):
    mean_sq = jnp.mean(rows * rows, axis=-1, keepdims=True)
    return rows * lax.rsqrt(mean_sq + EPS) * (1.0 + gain)


def solution(mesh):
    def local_fn(hidden, labels, gamma, table):
        mb_dev, seq_len, width = hidden.shape
        v_shard = table.shape[0]
        rank = lax.axis_index('pp')
        normed32, norm_vjp = jax.vjp(norm_rows, hidden.astype(jnp.float32), gamma)
        normed = normed32.astype(jnp.bfloat16)
        all_normed = lax.all_gather(normed, 'pp', axis=0, tiled=True)
        all_labels = lax.all_gather(labels, 'pp', axis=0, tiled=True)
        total = all_normed.shape[0] * seq_len
        vocab_ids = rank * v_shard + lax.broadcasted_iota(jnp.int32, (1, v_shard), 1)

        def micro_step(grad_table, scan_in):
            block, block_labels = scan_in
            logits = lax.dot_general(block, table, (((1,), (1,)), ((), ())), preferred_element_type=jnp.float32)
            tanh_z = jnp.tanh(logits / SOFT_CAP)
            capped = SOFT_CAP * tanh_z
            row_max = lax.pmax(jnp.max(capped, axis=1), 'pp')
            label_hit = vocab_ids == block_labels[:, None]
            shifted = jnp.exp(capped - row_max[:, None])
            local_stats = jnp.stack([jnp.sum(shifted, axis=1), jnp.sum(jnp.where(label_hit, capped, 0.0), axis=1)])
            group_stats = lax.psum(local_stats, 'pp')
            tok_loss = row_max + jnp.log(group_stats[0]) - group_stats[1]
            soft_probs = shifted / group_stats[0][:, None]
            grad_capped = jnp.where(label_hit, soft_probs - 1.0, soft_probs) / total
            grad_logits = (grad_capped * (1.0 - tanh_z * tanh_z)).astype(jnp.bfloat16)
            part_dn = jnp.dot(grad_logits, table, preferred_element_type=jnp.float32)
            table_part = lax.dot_general(grad_logits, block, (((0,), (0,)), ((), ())), preferred_element_type=jnp.float32)
            return grad_table + table_part, (tok_loss, part_dn)

        init_acc = jnp.zeros((v_shard, width), jnp.float32)
        grad_table, (all_loss, all_dn) = lax.scan(micro_step, init_acc, (all_normed, all_labels))
        own_dn = lax.psum_scatter(all_dn, 'pp', scatter_dimension=0, tiled=True)
        grad_rows, grad_gain = norm_vjp(own_dn)
        grad_gain = lax.psum(grad_gain, 'pp')
        own_loss = lax.dynamic_slice_in_dim(all_loss, rank * mb_dev, mb_dev, axis=0)
        mean_loss = jnp.reshape(jnp.mean(all_loss), (1,))
        return own_loss, grad_rows.astype(jnp.bfloat16), mean_loss, grad_table, grad_gain

    token_spec = P(('dp', 'pp'))
    return jax.shard_map(local_fn, mesh=mesh,
                         in_specs=(token_spec, token_spec, P(), P('pp')),
                         out_specs=(token_spec, token_spec, P('dp'), token_spec, P('dp')),
                         check_vma=False)
```

profile of v0, /device:TPU:21, one launch (start us, length us, event | category | flops | bytes accessed | tf_op | source)
XLA Modules:
  0.0 2876.9 jit_solution(4428045076173821892)
XLA Ops:
  36.5 84.0 %all-gather.3.cloned.1.call-done = bf16[32,512,576]{1,2,0:T(8,128)(2,1)} async-done(((bf16[2,512,576]{1,2,0:T(8,128)(2,1)}), bf16[32,512,576]{1,2,0:T(8,128)(2,1)}) %all-gather.3.cloned.1.call-update) | async-done | bytes 18874384 | tf_op jit(solution)/shard_map/all_gather | solution.py:22
  120.5 2515.5 %while.17 = (s32[]{:T(128)}, f32[3072,576]{0,1:T(8,128)}, f32[32,512]{1,0:T(8,128)S(1)}, f32[32,512,576]{1,2,0:T(8,128)}, s32[32,512]{1,0:T(8,128)S(1)}, /*index...) while((s32[]{:T(128)}, f32[3072,576]{0,1:T(8,128)}, ...), condition=%wide.region_7.8_spmd.clone, body=%wide.region_1.7_spmd.clone.sunk | while | flops 5492839424 | bytes 81905880 | solution.py:46
  157.0 24.9 psum.20
  205.8 23.6 pmax.12
  234.9 23.6 psum.20
  313.5 23.6 psum.20
  363.1 23.6 pmax.12
  392.2 23.6 psum.20
  441.7 23.6 pmax.12
  470.8 23.6 psum.20
  520.4 23.6 pmax.12
  549.4 23.6 psum.20
  628.1 23.6 psum.20
  677.7 23.6 pmax.12
  706.8 23.6 psum.20
  756.3 23.6 pmax.12
  785.4 23.6 psum.20
  834.9 23.6 pmax.12
  864.0 23.6 psum.20
  942.7 23.6 psum.20
  992.2 23.6 pmax.12
  1021.3 23.6 psum.20
  1070.9 23.6 pmax.12
  1099.9 23.6 psum.20
  1149.5 23.6 pmax.12
  1178.6 23.6 psum.20
  1228.2 23.6 pmax.12
  1257.3 23.6 psum.20
  1306.8 23.6 pmax.12
  1335.9 23.6 psum.20
  1414.6 23.6 psum.20
  1493.3 23.6 psum.20
  1571.9 23.6 psum.20
  1650.5 23.6 psum.20
  1729.2 23.6 psum.20
  1807.8 23.6 psum.20
  1886.5 23.6 psum.20
  1965.1 23.6 psum.20
  2043.7 23.6 psum.20
  2122.4 23.6 psum.20
  2201.0 23.6 psum.20
  2279.7 23.6 psum.20
  2358.3 23.6 psum.20
  2437.0 23.6 psum.20
  2515.6 23.6 psum.20
  2594.3 23.6 psum.20
  2638.0 200.3 %reduce-scatter.2.cloned.1.call-done = f32[2,512,576]{1,2,0:T(8,128)} async-done(((f32[32,512,576]{1,2,0:T(8,128)}), f32[2,512,576]{1,2,0:T(8,128)}) %reduce-scatter.2.cloned.1.call-update) | async-done | bytes 2359312 | tf_op jit(solution)/shard_map/reduce_scatter | solution.py:47
  2840.9 24.8 psum.17
  (596 shorter events, 1509.6 us)
Async XLA Ops:
  7.2 113.3 %all-gather.3.cloned.1.call-start = ((), (), s32[]{:S(2)}) async-start(), calls=%async_computation.1 | async-start | bytes 20054016 | tf_op jit(solution)/shard_map/all_gather | solution.py:22
  13.3 2825.0 %reduce-scatter.2.cloned.1.call-start = ((), (), s32[]{:S(2)}) async-start(), calls=%async_computation.2 | async-start | bytes 40108032 | tf_op jit(solution)/shard_map/reduce_scatter | solution.py:47
  151.5 40.8 %slice-start = ((s8[6291456]{0:T(1024)(128)(4,1)}), s8[2097152]{0:T(1024)(128)(4,1)S(1)}, s32[]{:S(2)}) async-start(s8[6291456]{0:T(1024)(128)(4,1)} %bitcast.48), calls=%async_computation.3 | async-start | bytes 4194304 | tf_op jit(solution)/shard_map/while
  229.4 41.5 %slice-start = ((s8[6291456]{0:T(1024)(128)(4,1)}), s8[2097152]{0:T(1024)(128)(4,1)S(1)}, s32[]{:S(2)}) async-start(s8[6291456]{0:T(1024)(128)(4,1)} %bitcast.48), calls=%async_computation.3 | async-start | bytes 4194304 | tf_op jit(solution)/shard_map/while
  308.1 41.5 %slice-start = ((s8[6291456]{0:T(1024)(128)(4,1)}), s8[2097152]{0:T(1024)(128)(4,1)S(1)}, s32[]{:S(2)}) async-start(s8[6291456]{0:T(1024)(128)(4,1)} %bitcast.48), calls=%async_computation.3 | async-start | bytes 4194304 | tf_op jit(solution)/shard_map/while
  386.7 41.5 %slice-start = ((s8[6291456]{0:T(1024)(128)(4,1)}), s8[2097152]{0:T(1024)(128)(4,1)S(1)}, s32[]{:S(2)}) async-start(s8[6291456]{0:T(1024)(128)(4,1)} %bitcast.48), calls=%async_computation.3 | async-start | bytes 4194304 | tf_op jit(solution)/shard_map/while
  465.3 41.5 %slice-start = ((s8[6291456]{0:T(1024)(128)(4,1)}), s8[2097152]{0:T(1024)(128)(4,1)S(1)}, s32[]{:S(2)}) async-start(s8[6291456]{0:T(1024)(128)(4,1)} %bitcast.48), calls=%async_computation.3 | async-start | bytes 4194304 | tf_op jit(solution)/shard_map/while
  544.0 41.5 %slice-start = ((s8[6291456]{0:T(1024)(128)(4,1)}), s8[2097152]{0:T(1024)(128)(4,1)S(1)}, s32[]{:S(2)}) async-start(s8[6291456]{0:T(1024)(128)(4,1)} %bitcast.48), calls=%async_computation.3 | async-start | bytes 4194304 | tf_op jit(solution)/shard_map/while
  573.2 12.3 slice-start.1
  622.6 41.5 %slice-start = ((s8[6291456]{0:T(1024)(128)(4,1)}), s8[2097152]{0:T(1024)(128)(4,1)S(1)}, s32[]{:S(2)}) async-start(s8[6291456]{0:T(1024)(128)(4,1)} %bitcast.48), calls=%async_computation.3 | async-start | bytes 4194304 | tf_op jit(solution)/shard_map/while
  701.3 41.5 %slice-start = ((s8[6291456]{0:T(1024)(128)(4,1)}), s8[2097152]{0:T(1024)(128)(4,1)S(1)}, s32[]{:S(2)}) async-start(s8[6291456]{0:T(1024)(128)(4,1)} %bitcast.48), calls=%async_computation.3 | async-start | bytes 4194304 | tf_op jit(solution)/shard_map/while
  779.9 41.5 %slice-start = ((s8[6291456]{0:T(1024)(128)(4,1)}), s8[2097152]{0:T(1024)(128)(4,1)S(1)}, s32[]{:S(2)}) async-start(s8[6291456]{0:T(1024)(128)(4,1)} %bitcast.48), calls=%async_computation.3 | async-start | bytes 4194304 | tf_op jit(solution)/shard_map/while
  809.1 12.3 slice-start.1
  858.6 41.5 %slice-start = ((s8[6291456]{0:T(1024)(128)(4,1)}), s8[2097152]{0:T(1024)(128)(4,1)S(1)}, s32[]{:S(2)}) async-start(s8[6291456]{0:T(1024)(128)(4,1)} %bitcast.48), calls=%async_computation.3 | async-start | bytes 4194304 | tf_op jit(solution)/shard_map/while
  937.2 41.5 %slice-start = ((s8[6291456]{0:T(1024)(128)(4,1)}), s8[2097152]{0:T(1024)(128)(4,1)S(1)}, s32[]{:S(2)}) async-start(s8[6291456]{0:T(1024)(128)(4,1)} %bitcast.48), calls=%async_computation.3 | async-start | bytes 4194304 | tf_op jit(solution)/shard_map/while
  1015.8 41.5 %slice-start = ((s8[6291456]{0:T(1024)(128)(4,1)}), s8[2097152]{0:T(1024)(128)(4,1)S(1)}, s32[]{:S(2)}) async-start(s8[6291456]{0:T(1024)(128)(4,1)} %bitcast.48), calls=%async_computation.3 | async-start | bytes 4194304 | tf_op jit(solution)/shard_map/while
  1045.0 12.3 slice-start.1
  1094.5 41.5 %slice-start = ((s8[6291456]{0:T(1024)(128)(4,1)}), s8[2097152]{0:T(1024)(128)(4,1)S(1)}, s32[]{:S(2)}) async-start(s8[6291456]{0:T(1024)(128)(4,1)} %bitcast.48), calls=%async_computation.3 | async-start | bytes 4194304 | tf_op jit(solution)/shard_map/while
  1173.1 41.5 %slice-start = ((s8[6291456]{0:T(1024)(128)(4,1)}), s8[2097152]{0:T(1024)(128)(4,1)S(1)}, s32[]{:S(2)}) async-start(s8[6291456]{0:T(1024)(128)(4,1)} %bitcast.48), calls=%async_computation.3 | async-start | bytes 4194304 | tf_op jit(solution)/shard_map/while
  1251.8 41.5 %slice-start = ((s8[6291456]{0:T(1024)(128)(4,1)}), s8[2097152]{0:T(1024)(128)(4,1)S(1)}, s32[]{:S(2)}) async-start(s8[6291456]{0:T(1024)(128)(4,1)} %bitcast.48), calls=%async_computation.3 | async-start | bytes 4194304 | tf_op jit(solution)/shard_map/while
  1330.4 41.5 %slice-start = ((s8[6291456]{0:T(1024)(128)(4,1)}), s8[2097152]{0:T(1024)(128)(4,1)S(1)}, s32[]{:S(2)}) async-start(s8[6291456]{0:T(1024)(128)(4,1)} %bitcast.48), calls=%async_computation.3 | async-start | bytes 4194304 | tf_op jit(solution)/shard_map/while
  1409.1 41.5 %slice-start = ((s8[6291456]{0:T(1024)(128)(4,1)}), s8[2097152]{0:T(1024)(128)(4,1)S(1)}, s32[]{:S(2)}) async-start(s8[6291456]{0:T(1024)(128)(4,1)} %bitcast.48), calls=%async_computation.3 | async-start | bytes 4194304 | tf_op jit(solution)/shard_map/while
  1438.3 12.3 slice-start.1
  1487.8 41.5 %slice-start = ((s8[6291456]{0:T(1024)(128)(4,1)}), s8[2097152]{0:T(1024)(128)(4,1)S(1)}, s32[]{:S(2)}) async-start(s8[6291456]{0:T(1024)(128)(4,1)} %bitcast.48), calls=%async_computation.3 | async-start | bytes 4194304 | tf_op jit(solution)/shard_map/while
  1517.0 12.3 slice-start.1
  1566.4 41.5 %slice-start = ((s8[6291456]{0:T(1024)(128)(4,1)}), s8[2097152]{0:T(1024)(128)(4,1)S(1)}, s32[]{:S(2)}) async-start(s8[6291456]{0:T(1024)(128)(4,1)} %bitcast.48), calls=%async_computation.3 | async-start | bytes 4194304 | tf_op jit(solution)/shard_map/while
  1645.1 41.5 %slice-start = ((s8[6291456]{0:T(1024)(128)(4,1)}), s8[2097152]{0:T(1024)(128)(4,1)S(1)}, s32[]{:S(2)}) async-start(s8[6291456]{0:T(1024)(128)(4,1)} %bitcast.48), calls=%async_computation.3 | async-start | bytes 4194304 | tf_op jit(solution)/shard_map/while
  1723.7 41.5 %slice-start = ((s8[6291456]{0:T(1024)(128)(4,1)}), s8[2097152]{0:T(1024)(128)(4,1)S(1)}, s32[]{:S(2)}) async-start(s8[6291456]{0:T(1024)(128)(4,1)} %bitcast.48), calls=%async_computation.3 | async-start | bytes 4194304 | tf_op jit(solution)/shard_map/while
  1752.9 12.3 slice-start.1
  1802.3 41.5 %slice-start = ((s8[6291456]{0:T(1024)(128)(4,1)}), s8[2097152]{0:T(1024)(128)(4,1)S(1)}, s32[]{:S(2)}) async-start(s8[6291456]{0:T(1024)(128)(4,1)} %bitcast.48), calls=%async_computation.3 | async-start | bytes 4194304 | tf_op jit(solution)/shard_map/while
  1831.5 12.3 slice-start.1
  1881.0 41.5 %slice-start = ((s8[6291456]{0:T(1024)(128)(4,1)}), s8[2097152]{0:T(1024)(128)(4,1)S(1)}, s32[]{:S(2)}) async-start(s8[6291456]{0:T(1024)(128)(4,1)} %bitcast.48), calls=%async_computation.3 | async-start | bytes 4194304 | tf_op jit(solution)/shard_map/while
  1959.6 41.5 %slice-start = ((s8[6291456]{0:T(1024)(128)(4,1)}), s8[2097152]{0:T(1024)(128)(4,1)S(1)}, s32[]{:S(2)}) async-start(s8[6291456]{0:T(1024)(128)(4,1)} %bitcast.48), calls=%async_computation.3 | async-start | bytes 4194304 | tf_op jit(solution)/shard_map/while
  1988.8 12.3 slice-start.1
  2038.3 41.5 %slice-start = ((s8[6291456]{0:T(1024)(128)(4,1)}), s8[2097152]{0:T(1024)(128)(4,1)S(1)}, s32[]{:S(2)}) async-start(s8[6291456]{0:T(1024)(128)(4,1)} %bitcast.48), calls=%async_computation.3 | async-start | bytes 4194304 | tf_op jit(solution)/shard_map/while
  2067.5 12.3 slice-start.1
  2116.9 41.5 %slice-start = ((s8[6291456]{0:T(1024)(128)(4,1)}), s8[2097152]{0:T(1024)(128)(4,1)S(1)}, s32[]{:S(2)}) async-start(s8[6291456]{0:T(1024)(128)(4,1)} %bitcast.48), calls=%async_computation.3 | async-start | bytes 4194304 | tf_op jit(solution)/shard_map/while
  2195.5 41.5 %slice-start = ((s8[6291456]{0:T(1024)(128)(4,1)}), s8[2097152]{0:T(1024)(128)(4,1)S(1)}, s32[]{:S(2)}) async-start(s8[6291456]{0:T(1024)(128)(4,1)} %bitcast.48), calls=%async_computation.3 | async-start | bytes 4194304 | tf_op jit(solution)/shard_map/while
  2274.2 41.5 %slice-start = ((s8[6291456]{0:T(1024)(128)(4,1)}), s8[2097152]{0:T(1024)(128)(4,1)S(1)}, s32[]{:S(2)}) async-start(s8[6291456]{0:T(1024)(128)(4,1)} %bitcast.48), calls=%async_computation.3 | async-start | bytes 4194304 | tf_op jit(solution)/shard_map/while
  2352.8 41.5 %slice-start = ((s8[6291456]{0:T(1024)(128)(4,1)}), s8[2097152]{0:T(1024)(128)(4,1)S(1)}, s32[]{:S(2)}) async-start(s8[6291456]{0:T(1024)(128)(4,1)} %bitcast.48), calls=%async_computation.3 | async-start | bytes 4194304 | tf_op jit(solution)/shard_map/while
  2431.5 41.5 %slice-start = ((s8[6291456]{0:T(1024)(128)(4,1)}), s8[2097152]{0:T(1024)(128)(4,1)S(1)}, s32[]{:S(2)}) async-start(s8[6291456]{0:T(1024)(128)(4,1)} %bitcast.48), calls=%async_computation.3 | async-start | bytes 4194304 | tf_op jit(solution)/shard_map/while
  2510.1 41.5 %slice-start = ((s8[6291456]{0:T(1024)(128)(4,1)}), s8[2097152]{0:T(1024)(128)(4,1)S(1)}, s32[]{:S(2)}) async-start(s8[6291456]{0:T(1024)(128)(4,1)} %bitcast.48), calls=%async_computation.3 | async-start | bytes 4194304 | tf_op jit(solution)/shard_map/while
  2539.3 12.3 slice-start.1
  2588.8 41.5 %slice-start = ((s8[6291456]{0:T(1024)(128)(4,1)}), s8[2097152]{0:T(1024)(128)(4,1)S(1)}, s32[]{:S(2)}) async-start(s8[6291456]{0:T(1024)(128)(4,1)} %bitcast.48), calls=%async_computation.3 | async-start | bytes 4194304 | tf_op jit(solution)/shard_map/while
  2636.0 202.3 %copy-start.1 = (bf16[2,512,576]{1,2,0:T(8,128)(2,1)S(1)}, bf16[2,512,576]{1,2,0:T(8,128)(2,1)}, u32[]{:S(2)}) copy-start(bf16[2,512,576]{1,2,0:T(8,128)(2,1)} %param.6) | copy-start | bytes 3538948
  2636.0 202.3 %copy-start.3 = (f32[576]{0:T(1024)S(1)}, f32[576]{0:T(1024)}, u32[]{:S(2)}) copy-start(f32[576]{0:T(1024)} %copy-done.2) | copy-start | bytes 6916
  2636.1 202.3 %copy-start.5 = (f32[2,512]{1,0:T(2,128)S(1)}, f32[2,512]{1,0:T(2,128)}, u32[]{:S(2)}) copy-start(f32[2,512]{1,0:T(2,128)} %copy-done.4) | copy-start | bytes 12292
  2636.1 229.6 %copy-start.7 = (f32[2,512]{1,0:T(2,128)S(1)}, f32[2,512]{1,0:T(2,128)}, u32[]{:S(2)}) copy-start(f32[2,512]{1,0:T(2,128)} %copy-done.6) | copy-start | bytes 12292
  (57 other events, 664.8 us)
Sparse Core Ops, SparseCore 0:
  13.4 107.0 all-gather.2
  2636.2 202.0 reduce-scatter.1
where the time goes:
time: 2880 us
  blocking collectives  1560 us (54%)
  matrix products  823 us (29%)
  waiting for transfers between devices  284 us (10%)
  other arithmetic  187 us (6%)
    psum x32, blocking collectives, micro_step(): group_stats = lax.psum(local_stats, 'pp')  757 us
    pmax x32, blocking collectives, micro_step(): row_max = lax.pmax(jnp.max(capped, axis=1), 'pp')  755 us
    dot_general x32, matrix products, micro_step(): lax.dot_general(grad_logits, block, (((0,), (0,)), ((), ())), preferred_e...  392 us
    dot_general x32, matrix products, micro_step(): lax.dot_general(block, table, (((1,), (1,)), ((), ())), preferred_element...  249 us
    reduce_scatter x1, waiting for transfers between devices, local_fn(): own_dn = lax.psum_scatter(all_dn, 'pp', scatter_dimension=0, tiled=True)  200 us
    dot_general x32, matrix products, micro_step(): part_dn = jnp.dot(grad_logits, table, preferred_element_type=jnp.float32)  182 us
    reduce_sum x32, other arithmetic, micro_step(): jnp.sum(shifted, axis=1)  175 us
    all_gather x1, waiting for transfers between devices, local_fn(): all_normed = lax.all_gather(normed, 'pp', axis=0, tiled=True)  84 us
  transfers between devices with their start and end apart: 2, of which 2 were waited for; matrix products, arithmetic and copies ran while one was open for 0% of the time, Pallas kernels for 0%

commit v1 on v0

v1 whole, which is shorter than its diff:
```python
import functools
import math

import jax
import jax.numpy as jnp
from jax import lax
from jax.experimental import pallas as pl
from jax.experimental.pallas import tpu as pltpu
from jax.sharding import PartitionSpec as P

F32, BF16 = jnp.float32, jnp.bfloat16
SOFT_CAP = 30.0
EXP2_SCALE = SOFT_CAP * math.log2(math.e)
MESH = pl.DeviceIdType.MESH
TILE = 256
TB = 2 * TILE
CH = 256
FR = 192
PAD_ROWS = 8
VC = 3072
VB = 3072
Q = (0, 1)


def lanes(q):
    return pl.ds(q * TILE, TILE)


def run_stream(items, ahead):
    vals = {}
    for i in range(len(items) + ahead):
        if i < len(items):
            vals[i] = items[i][0]()
        if i >= ahead:
            items[i - ahead][1](vals.pop(i - ahead))


def kernel(n_pp, nb, per, total, V, D, n_hbm, lab, W, WT, dW_in, dn_hbm, dW_out, s_out,
           U, nbuf, dW, dnb, labm, svec, own, rbuf,
           n_sem, o_sem, w_sem, send_sem, recv_sem):
    tc = n_hbm.shape[2]
    me = lax.axis_index("pp")

    def peer(k):
        return {"pp": lax.rem(me + k, n_pp)}

    def n_copies(i):
        slot = lax.rem(i, 3)
        return [pltpu.make_async_copy(n_hbm.at[i * per + a],
                                      nbuf.at[slot, :, pl.ds(a * tc, tc)], n_sem.at[slot, a])
                for a in range(per)]

    def dn_copies(i):
        slot = lax.rem(i, 2)
        return [pltpu.make_async_copy(dnb.at[slot, :, pl.ds(a * tc, tc)],
                                      dn_hbm.at[i * per + a], o_sem.at[slot, a])
                for a in range(per)]

    def stat_copy(i, k):
        return pltpu.make_async_remote_copy(
            src_ref=own.at[i], dst_ref=rbuf.at[i, me], send_sem=send_sem.at[i, k - 1],
            recv_sem=recv_sem.at[i, n_pp - 1 - k], device_id=peer(k), device_id_type=MESH)

    w_load = pltpu.make_async_copy(dW_in, dW, w_sem)
    w_load.start()
    for c in n_copies(0):
        c.start()
    if n_pp > 1:
        barrier = pltpu.get_barrier_semaphore()
        for k in range(1, n_pp):
            pl.semaphore_signal(barrier, inc=1, device_id=peer(k), device_id_type=MESH)
        pl.semaphore_wait(barrier, n_pp - 1)
    base = me * V

    def f_part(slot, nF, c, st):
        rows = pl.ds(pl.multiple_of(c * VC, VC), VC)
        z = jnp.dot(W[rows, :], nF[...], preferred_element_type=F32)
        t = jnp.tanh(z * (1.0 / SOFT_CAP))
        U[slot, rows, :] = t
        return st + jnp.sum(jnp.exp2(t * EXP2_SCALE).reshape(VC // 8, 8, TB), axis=0)

    def b_part(slot, nB, c, tl):
        rows = pl.ds(pl.multiple_of(c * VB, VB), VB)
        t = U[slot, rows, :]
        p = jnp.exp2(t * EXP2_SCALE) * svec[0:1, :]
        hit = lax.broadcasted_iota(jnp.int32, (VB, TB), 0) == labm[0:1, :] - c * VB
        tl = tl + jnp.sum(jnp.where(hit, t, 0.0).reshape(VB // 8, 8, TB), axis=0)
        g = p - jnp.where(hit, 1.0 / total, 0.0)
        dz = (g * (1.0 - t * t)).astype(BF16)
        return dz, tl

    def b_dots(slot, nB, c, dz):
        part = jnp.dot(WT[:, pl.ds(pl.multiple_of(c * VB, VB), VB)], dz, preferred_element_type=F32)
        cols = pl.ds(pl.multiple_of(c * VB, VB), VB)
        dW[:, cols] += lax.dot_general(nB[...], dz, (((1,), (1,)), ((), ())), preferred_element_type=F32)
        return part

    def fwd_start(i):
        for c in n_copies(i):
            c.wait()

        @pl.when(i + 1 < nb)
        def _():
            for c in n_copies(i + 1):
                c.start()

    def fwd_end(i, st):
        own[i] = jnp.sum(st, axis=0, keepdims=True)
        for k in range(1, n_pp):
            stat_copy(i, k).start()

    def bwd_start(i):
        for k in range(1, n_pp):
            stat_copy(i, k).wait_recv()
        acc = jnp.zeros((1, TB), F32)
        for k in range(n_pp):
            acc = acc + (jnp.where(k == me, own[i], rbuf[i, k]) if n_pp > 1 else own[i])
        s_out[i] = acc
        svec[...] = jnp.broadcast_to(1.0 / (acc * total), (8, TB))
        labm[...] = jnp.broadcast_to(lab[i] - base, (8, TB))

        @pl.when(i >= 2)
        def _():
            for c in dn_copies(i - 2):
                c.wait()

    def bwd_end(i, tl):
        dnb[lax.rem(i, 2), pl.ds(D, PAD_ROWS), :] = tl
        for c in dn_copies(i):
            c.start()
        for k in range(1, n_pp):
            stat_copy(i, k).wait_send()

    z8 = jnp.zeros((8, TB), F32)

    def step(i, _):
        @pl.when(i < nb)
        def _():
            fwd_start(i)
            slot, nF = lax.rem(i, 2), nbuf.at[lax.rem(i, 3)]
            st = lax.fori_loop(0, V // VC, lambda c, st: f_part(slot, nF, c, st), z8)
            fwd_end(i, st)

        @pl.when(i == 0)
        def _():
            w_load.wait()

        @pl.when(i > 0)
        def _():
            bwd_start(i - 1)
            slot, nB = lax.rem(i - 1, 2), nbuf.at[lax.rem(i - 1, 3)]
            dn = dnb.at[slot]

            def body(c, tl):
                dz, tl = b_part(slot, nB, c, tl)
                part = b_dots(slot, nB, c, dz)
                @pl.when(c == 0)
                def _():
                    dn[0:D, :] = part

                @pl.when(c > 0)
                def _():
                    dn[0:D, :] += part
                return tl
            if V // VB == 1:
                dz, tl = b_part(slot, nB, 0, z8)
                dn[0:D, :] = b_dots(slot, nB, 0, dz)
            else:
                dn[...] = jnp.zeros((D + PAD_ROWS, TB), F32)
                def body2(c, tl):
                    dz, tl = b_part(slot, nB, c, tl)
                    dn[0:D, :] += b_dots(slot, nB, c, dz)
                    return tl
                tl = lax.fori_loop(0, V // VB, body2, z8)
            bwd_end(i - 1, tl)
        return 0
    lax.fori_loop(0, nb + 1, step, 0)
    w_store = pltpu.make_async_copy(dW, dW_out, w_sem)
    w_store.start()
    for i in (nb - 2, nb - 1):
        for c in dn_copies(i):
            c.wait()
    w_store.wait()


def chunk_call(n_all, lab, W, WT, dW, *, n_pp, total, cid):
    D, V = WT.shape
    g, _, tc = n_all.shape
    per = TB // tc
    nb = g // per
    hbm = pl.BlockSpec(memory_space=pl.ANY)
    vmem = pl.BlockSpec(memory_space=pltpu.VMEM)
    nk = max(n_pp - 1, 1)
    return pl.pallas_call(
        functools.partial(kernel, n_pp, nb, per, float(total), V, D),
        out_shape=[jax.ShapeDtypeStruct((g, D + PAD_ROWS, tc), F32), jax.ShapeDtypeStruct((D, V), F32),
                   jax.ShapeDtypeStruct((nb, 1, TB), F32)],
        in_specs=[hbm, vmem, vmem, vmem, hbm],
        out_specs=[hbm, hbm, vmem],
        scratch_shapes=[
            pltpu.VMEM((2, V, TB), F32),
            pltpu.VMEM((3, D, TB), BF16), pltpu.VMEM((D, V), F32), pltpu.VMEM((2, D + PAD_ROWS, TB), F32),
            pltpu.VMEM((8, TB), jnp.int32), pltpu.VMEM((8, TB), F32),
            pltpu.VMEM((nb, 1, TB), F32), pltpu.VMEM((nb, n_pp, 1, TB), F32),
            pltpu.SemaphoreType.DMA((3, per)), pltpu.SemaphoreType.DMA((2, per)), pltpu.SemaphoreType.DMA,
            pltpu.SemaphoreType.DMA((nb, nk)), pltpu.SemaphoreType.DMA((nb, nk)),
        ],
        input_output_aliases={4: 1},
        compiler_params=pltpu.CompilerParams(
            vmem_limit_bytes=56 * 1024 * 1024,
            **(dict(collective_id=cid, has_side_effects=True) if n_pp > 1 else {})),
        cost_estimate=pl.CostEstimate(flops=6 * g * tc * D * V, bytes_accessed=g * tc * D * 6 + D * V * 8, transcendentals=0),
        name=f"core{cid}",
    )(n_all, lab, W, WT, dW)


def sum_kernel(n_pp, x_ref, o_ref, rbuf, send_sem, recv_sem):
    me = lax.axis_index("pp")

    def peer(k):
        return {"pp": lax.rem(me + k, n_pp)}

    barrier = pltpu.get_barrier_semaphore()
    for k in range(1, n_pp):
        pl.semaphore_signal(barrier, inc=1, device_id=peer(k), device_id_type=MESH)
    pl.semaphore_wait(barrier, n_pp - 1)
    copies = [pltpu.make_async_remote_copy(
        src_ref=x_ref, dst_ref=rbuf.at[me], send_sem=send_sem.at[k - 1], recv_sem=recv_sem.at[n_pp - 1 - k],
        device_id=peer(k), device_id_type=MESH) for k in range(1, n_pp)]
    for c in copies:
        c.start()
    for c in copies:
        c.wait_recv()
    acc = jnp.zeros_like(o_ref)
    for k in range(n_pp):
        acc = acc + jnp.where(k == me, x_ref[...], rbuf[k])
    o_ref[...] = acc
    for c in copies:
        c.wait_send()


def small_sum(x, n_pp, cid):
    vmem = pl.BlockSpec(memory_space=pltpu.VMEM)
    return pl.pallas_call(
        functools.partial(sum_kernel, n_pp), out_shape=jax.ShapeDtypeStruct(x.shape, F32),
        in_specs=[vmem], out_specs=vmem,
        scratch_shapes=[pltpu.VMEM((n_pp,) + x.shape, F32), pltpu.SemaphoreType.DMA((n_pp - 1,)),
                        pltpu.SemaphoreType.DMA((n_pp - 1,))],
        compiler_params=pltpu.CompilerParams(collective_id=cid, has_side_effects=True), name="small_sum")(x)


EPS = 1e-6
WIDTHS = (256, 512, 256)


def norm_cols(cols, gain):
    mean_sq = jnp.mean(cols * cols, axis=1, keepdims=True)
    return cols * lax.rsqrt(mean_sq + EPS) * (1.0 + gain)[None, :, None]


def solution(mesh):
    n_pp = mesh.shape["pp"]

    def local_fn(hidden, labels, gamma, table):
        mb, seq, D = hidden.shape
        V = table.shape[0]
        T = mb * seq
        total = T * n_pp
        me = lax.axis_index("pp")
        cols = jnp.swapaxes(hidden, 1, 2).astype(F32)
        normed, norm_vjp = jax.vjp(norm_cols, cols, gamma)
        normed = jnp.concatenate(list(normed.astype(BF16)), axis=1)
        starts = [sum(WIDTHS[:k]) for k in range(len(WIDTHS))]
        gathered = [lax.all_gather(normed[:, a:a + w], "pp", axis=0) for a, w in zip(starts, WIDTHS)]
        all_labels = lax.all_gather(labels.reshape(T), "pp", axis=0)
        WT = table.T
        dW = jnp.zeros(WT.shape, F32)
        dn_own, sums = [], []
        for k, (a, w) in enumerate(zip(starts, WIDTHS)):
            lab = all_labels[:, a:a + w].reshape(n_pp * w // TB, 1, TB)
            dn, dW, s = chunk_call(gathered[k], lab, table, WT, dW, n_pp=n_pp, total=total, cid=k + 1)
            dn_own.append(lax.psum_scatter(dn, "pp", scatter_dimension=0, tiled=False))
            sums.append(lax.dynamic_index_in_dim(s.reshape(n_pp, w), me, 0, keepdims=False))
        dn = jnp.concatenate(dn_own, axis=1)
        loss = jnp.log(jnp.concatenate(sums)) - SOFT_CAP * jnp.sum(dn[D:], axis=0)
        d_cols, d_gain = norm_vjp(dn[:D].reshape(D, mb, seq).swapaxes(0, 1))
        flat = jnp.concatenate([d_gain, jnp.sum(loss)[None]])
        rows = -(-flat.shape[0] // 1024) * 8
        flat = jnp.pad(flat, (0, rows * 128 - flat.shape[0])).reshape(rows, 128)
        flat = small_sum(flat, n_pp, len(WIDTHS) + 1).reshape(-1)
        return (loss.reshape(mb, seq), jnp.swapaxes(d_cols, 1, 2).astype(BF16), flat[D:D + 1] / total,
                dW.T, flat[:D])

    token_spec = P(("dp", "pp"))
    return jax.shard_map(local_fn, mesh=mesh,
                         in_specs=(token_spec, token_spec, P(), P("pp")),
                         out_specs=(token_spec, token_spec, P("dp"), token_spec, P("dp")),
                         check_vma=False)
```

time: 2880 us -> 598 us (0.21)
  blocking collectives: 1560 us -> 23.1 us
  matrix products: 823 us -> 0 us
  Pallas kernels: 0 us -> 332 us
  other arithmetic: 187 us -> 10.2 us
  waiting for transfers between devices: 284 us -> 189 us
    dot_general x96 -> x0, matrix products: 823 us -> none  [the longest x32 392 us: micro_step(): lax.dot_general(grad_logits, block, (((0,), (0,)), ((), ())), preferred_e...]
    psum x33 -> x0, blocking collectives: 782 us -> none  [the longest x32 757 us: micro_step(): group_stats = lax.psum(local_stats, 'pp')]
    pmax x32 -> x0, blocking collectives: 755 us -> none  [micro_step(): row_max = lax.pmax(jnp.max(capped, axis=1), 'pp')]
    pallas_call x0 -> x4, Pallas kernels: none -> 332 us  [the longest x3 322 us: chunk_call(): pl.pallas_call(functools.partial(kernel, n_pp, nb, per, float(total), V,...]
    reduce_sum x35 -> x4, other arithmetic: 179 us -> 3.88 us  [the longest x1 1.53 us: norm_cols(): mean_sq = jnp.mean(cols * cols, axis=1, keepdims=True)]
    all_gather x1 -> x3, waiting for transfers between devices: 84 us -> 12.4 us  [local_fn(): lax.all_gather(normed[:, a:a + w], 'pp', axis=0)]
    reduce_scatter x1 -> x3, waiting for transfers between devices: 200 us -> 176 us  [local_fn(): dn_own.append(lax.psum_scatter(dn, 'pp', scatter_dimension=0, tiled=False))]
  transfers between devices with their start and end apart: 2 -> 6, of which waited for: 2 -> 3; matrix products, arithmetic and copies ran while one was open for 0% -> 3% of each run, Pallas kernels for 0% -> 54%
where the time goes in v1:
time: 598 us; the launch traced here: 597 us
  Pallas kernels  332 us (56%)
  waiting for transfers between devices  189 us (32%)
  local copies, waits for them, and re-layouts  26.2 us (4%)
  blocking collectives  23.1 us (4%)
  between operations  16.2 us (3%)
  other arithmetic  10.2 us (2%)
    pallas_call x3, Pallas kernels, chunk_call(): pl.pallas_call(functools.partial(kernel, n_pp, nb, per, float(total), V,...  322 us
    reduce_scatter x3, waiting for transfers between devices, local_fn(): dn_own.append(lax.psum_scatter(dn, 'pp', scatter_dimension=0, tiled=False))  176 us
    all_gather x1, blocking collectives, local_fn(): all_labels = lax.all_gather(labels.reshape(T), 'pp', axis=0)  23.1 us
    unnamed x39, local copies, waits for them, and re-layouts  15.5 us
    all_gather x3, waiting for transfers between devices, local_fn(): lax.all_gather(normed[:, a:a + w], 'pp', axis=0)  12.4 us
  transfers between devices with their start and end apart: 6, of which 3 were waited for; matrix products, arithmetic and copies ran while one was open for 3% of the time, Pallas kernels for 54%

profile of v1, /device:TPU:21, one launch (start us, length us, event | category | flops | bytes accessed | tf_op | source)
XLA Modules:
  0.0 597.5 jit_solution(4072465909567347984)
XLA Ops:
  7.2 0.1 all-gather.8.cloned.1.call-start
  7.2 0.7 broadcast_add_fusion
  7.9 1.5 fusion.7
  9.5 0.6 copy-done.8
  10.1 1.6 fusion.5
  11.7 0.1 slice_bitcast_fusion.1
  11.8 0.7 slice.40
  12.6 0.1 all-gather.10.cloned.1.call-start
  12.6 0.9 pad_maximum_fusion.2
  13.5 0.1 all-gather.10.cloned.1.call-update
  13.6 0.1 all-gather.12.cloned.1.call-start
  13.6 0.7 slice.43
  14.4 0.1 reduce-scatter.4.cloned.1.call-start
  14.5 23.1 %all-gather.3 = s32[16,1,1024]{2,1,0:T(1,128)S(1)} all-gather(s32[1,1,1024]{2,1,0:T(1,128)S(1)} %reshape.75), channel_id=1, replica_groups=mesh['dp'=4,'pp'=16] {'pp'}, dimensions={0}, use_global_device_ids=true | all-gather | bytes 69632 | tf_op jit(solution)/shard_map/all_gather | solution.py:275
  37.6 0.6 reshape.78.lab
  38.2 6.1 %copy.19.W = bf16[3072,576]{1,0:T(8,128)(2,1)} copy(bf16[3072,576]{0,1:T(8,128)(2,1)} %param.7) | data formatting | bytes 7077888 | tf_op args[3]
  44.3 12.4 %all-gather.8.cloned.1.call-done = bf16[9216,256]{1,0:T(8,128)(2,1)} async-done(((bf16[576,256]{1,0:T(8,128)(2,1)}), bf16[9216,256]{1,0:T(8,128)(2,1)}) %all-gather.8.cloned.1.call-update) | async-done | bytes 4718608 | tf_op jit(solution)/shard_map/all_gather | solution.py:274
  56.7 3.7 broadcast_in_dim.11.dW_in
  60.4 83.3 %core1.1 = (f32[16,584,256]{2,1,0:T(8,128)}, f32[576,3072]{1,0:T(8,128)}, f32[8,1,512]{2,1,0:T(1,128)}) custom-call(bf16[16,576,256]{2,1,0:T(8,128)(2,1)} %bitcast.92, s32[8,1,512]{2,1,0:T(1,128)} %reshape.78.lab, bf16[3072,576]{1,0:T(8,128)(2,1)} %copy.19.W, bf16[576,3072]{1,0:T(8,128)(2,1)} %bitcast.76, ...), custom_call_target="tpu_custom_call", output_to_operand_aliasing={{1}: (4, {})} | custom-call | flops 43486543872 | bytes 28311552 | tf_op jit(solution)/shard_map/core1/pallas_call | solution.py:194
  143.7 0.1 reduce-scatter.4.cloned.1.call-update
  143.8 0.2 reduce-scatter.8.cloned.1.call-start
  144.1 0.6 reshape.66.lab
  144.7 0.6 reshape.67.lab
  145.3 155.7 %core2.1 = (f32[16,584,512]{2,1,0:T(8,128)}, f32[576,3072]{1,0:T(8,128)}, f32[16,1,512]{2,1,0:T(1,128)}) custom-call(bf16[16,576,512]{2,1,0:T(8,128)(2,1)} %bitcast.90, s32[16,1,512]{2,1,0:T(1,128)} %reshape.66.lab, bf16[3072,576]{1,0:T(8,128)(2,1)} %copy.19.W, bf16[576,3072]{1,0:T(8,128)(2,1)} %bitcast.77, ...), custom_call_target="tpu_custom_call", output_to_operand_aliasing={{1}: (4, {})} | custom-call | flops 86973087744 | bytes 42467328 | tf_op jit(solution)/shard_map/core2/pallas_call | solution.py:194
  301.0 83.0 %core3.1 = (f32[16,584,256]{2,1,0:T(8,128)}, f32[576,3072]{1,0:T(8,128)}, f32[8,1,512]{2,1,0:T(1,128)}) custom-call(bf16[16,576,256]{2,1,0:T(8,128)(2,1)} %bitcast.91, s32[8,1,512]{2,1,0:T(1,128)} %reshape.67.lab, bf16[3072,576]{1,0:T(8,128)(2,1)} %copy.19.W, bf16[576,3072]{1,0:T(8,128)(2,1)} %bitcast.78, ...), custom_call_target="tpu_custom_call", output_to_operand_aliasing={{1}: (4, {})} | custom-call | flops 43486543872 | bytes 28311552 | tf_op jit(solution)/shard_map/core3/pallas_call | solution.py:194
  384.1 0.1 reduce-scatter.8.cloned.1.call-update
  384.1 0.1 reduce-scatter.6.cloned.1.call-start
  384.2 0.5 reduce-scatter.6.cloned.1.call-update
  384.8 0.1 copy-done.10
  385.0 1.2 constant_dynamic-slice_fusion.1
  386.2 0.6 constant_dynamic-slice_fusion
  386.8 63.0 %reduce-scatter.8.cloned.1.call-done = f32[1,584,256]{2,1,0:T(8,128)} async-done(((f32[16,584,256]{2,1,0:T(8,128)}), f32[1,584,256]{2,1,0:T(8,128)}) %reduce-scatter.8.cloned.1.call-update) | async-done | bytes 598032 | tf_op jit(solution)/shard_map/reduce_scatter | solution.py:282
  449.8 112.6 %reduce-scatter.6.cloned.1.call-done = f32[1,584,512]{2,1,0:T(8,128)} async-done(((f32[16,584,512]{2,1,0:T(8,128)}), f32[1,584,512]{2,1,0:T(8,128)}) %reduce-scatter.6.cloned.1.call-update) | async-done | bytes 1196048 | tf_op jit(solution)/shard_map/reduce_scatter | solution.py:282
  562.4 0.9 maximum_reduce_fusion
  563.3 0.4 copy-done.1
  563.7 0.1 copy-done.2
  563.9 0.2 copy-done.3
  564.1 0.3 pad_maximum_fusion
  564.4 0.4 copy-done.13
  564.8 0.6 fusion.16
  565.4 0.6 sub.8
  566.0 0.8 fusion.6
  566.9 1.3 fusion.13.x_ref
  568.2 10.4 %small_sum.1 = f32[8,128]{1,0:T(8,128)} custom-call(f32[8,128]{1,0:T(8,128)} %fusion.13.x_ref), custom_call_target="tpu_custom_call" | custom-call | tf_op jit(solution)/shard_map/small_sum/pallas_call | solution.py:244
  578.6 1.3 slice.38
  579.9 1.6 fusion.9
  582.1 6.8 %copy.36 = f32[3072,576]{0,1:T(8,128)} copy(f32[3072,576]{0,1:T(8,128)} %bitcast.71) | data formatting | bytes 14155776
  588.9 0.6 copy.37
  (43 shorter events, 0.4 us)
Async XLA Ops:
  7.2 49.5 %all-gather.8.cloned.1.call-start = ((), (), s32[]{:S(2)}) async-start(), calls=%async_computation.6 | async-start | bytes 5013504 | tf_op jit(solution)/shard_map/all_gather | solution.py:274
  7.9 3.8 copy-start.4
  9.5 0.6 copy-start.8
  10.1 1.7 copy-start.6
  11.8 2.7 copy-start.14
  12.6 132.8 %all-gather.10.cloned.1.call-start = ((), (), s32[]{:S(2)}) async-start(), calls=%async_computation.7 | async-start | bytes 10027008 | tf_op jit(solution)/shard_map/all_gather | solution.py:274
  13.6 287.5 %all-gather.12.cloned.1.call-start = ((), (), s32[]{:S(2)}) async-start(), calls=%async_computation.8 | async-start | bytes 5013504 | tf_op jit(solution)/shard_map/all_gather | solution.py:274
  14.4 372.4 %reduce-scatter.4.cloned.1.call-start = ((), (), s32[]{:S(2)}) async-start(), calls=%async_computation.3 | async-start | bytes 10166272 | tf_op jit(solution)/shard_map/reduce_scatter | solution.py:282
  143.8 306.0 %reduce-scatter.8.cloned.1.call-start = ((), (), s32[]{:S(2)}) async-start(), calls=%async_computation.5 | async-start | bytes 10166272 | tf_op jit(solution)/shard_map/reduce_scatter | solution.py:282
  384.1 178.3 %reduce-scatter.6.cloned.1.call-start = ((), (), s32[]{:S(2)}) async-start(), calls=%async_computation.4 | async-start | bytes 20332544 | tf_op jit(solution)/shard_map/reduce_scatter | solution.py:282
  384.2 0.7 copy-start.10
  384.2 0.8 copy-start.11
  562.4 1.3 copy-start.1
  562.4 1.5 copy-start.2
  562.4 1.6 copy-start.3
  564.1 0.7 copy-start.13
  564.1 0.7 copy-start.15
  564.1 0.7 copy-start.16
  564.1 1.9 copy-start
  564.1 1.9 copy-start.5
  564.1 1.9 copy-start.7
  564.4 15.5 %copy-start.9 = (f32[2,512]{1,0:T(2,128)S(1)}, f32[2,512]{1,0:T(2,128)}, u32[]{:S(2)}) copy-start(f32[2,512]{1,0:T(2,128)} %copy-done.8) | copy-start | bytes 12292
  582.1 6.8 %copy-start.12 = (f32[8,128]{1,0:T(8,128)S(1)}, f32[8,128]{1,0:T(8,128)}, u32[]{:S(2)}) copy-start(f32[8,128]{1,0:T(8,128)} %small_sum.1) | copy-start | bytes 12292
Sparse Core Ops, SparseCore 0:
  12.7 43.9 all-gather.7
  58.9 60.5 all-gather.9
  121.2 38.0 all-gather.11
  161.5 69.8 reduce-scatter.3
  384.2 65.5 reduce-scatter.7
  452.0 110.3 reduce-scatter.5

commit v2 on v0

v2 whole, which is shorter than its diff:
```python
import functools
import math

import jax
import jax.numpy as jnp
from jax import lax
from jax.experimental import pallas as pl
from jax.experimental.pallas import tpu as pltpu
from jax.sharding import PartitionSpec as P

F32, BF16 = jnp.float32, jnp.bfloat16
SOFT_CAP = 30.0
EPS = 1e-6
EXP2_SCALE = SOFT_CAP * math.log2(math.e)
MESH = pl.DeviceIdType.MESH
CORES = 2
LANE = 128
TILES = 4
TB = LANE * TILES
HALF = TB // CORES
PAD_ROWS = 8
HOPS = (4, 3)


def kernel(n_pp, total, n_own, lab_own, W, WT,
           dn_out, dW_out, s_out, n_all, dnp, prx,
           U, nblk, dW, dnb, svec, labm, lab_all, own_s, x1, x2, Sb, rx, ownv, sendb, outv,
           ag_recv, ag_send, pag_recv, pag_send, pair_recv, pair_send, dnp_sem, ring_recv, ring_send,
           st_recv, st_send, lab_recv, lab_send, nl_sem, ov_sem, io_sem):
    D, T = n_own.shape
    V = W.shape[0]
    D8 = D + PAD_ROWS
    nz = n_pp // CORES
    nsb = T // LANE
    per_sb = n_pp // TILES
    nb = nsb * per_sb
    me = lax.axis_index("pp")
    z, core = me // CORES, lax.rem(me, CORES)

    def dev(chip, c=core):
        return lax.rem(chip + 2 * nz, nz) * CORES + c

    def at(index):
        return {"pp": index}

    partner = at(z * CORES + 1 - core)

    def lanes_of(sb):
        return pl.ds(pl.multiple_of(sb * LANE, LANE), LANE)

    def remote(src, dst, ssem, rsem, where):
        return pltpu.make_async_remote_copy(src_ref=src, dst_ref=dst, send_sem=ssem, recv_sem=rsem,
                                            device_id=where, device_id_type=MESH)

    def sign(sb, d):
        g = 1 - 2 * lax.rem(sb, 2)
        return g if d == 0 else -g

    def ag_ring(sb, d, r):
        g = sign(sb, d)
        if r == 0:
            src = n_own.at[:, lanes_of(sb)]
        else:
            src = n_all.at[dev(z - g * r), :, lanes_of(sb)]
        return remote(src, n_all.at[dev(z - g * r), :, lanes_of(sb)], ag_send.at[sb, d, r], ag_recv.at[sb, d, r],
                      at(dev(z + g)))

    def ag_partner(sb, chip, own=False):
        i = lax.rem(chip + 2 * nz, nz)
        src = n_own.at[:, lanes_of(sb)] if own else n_all.at[dev(chip), :, lanes_of(sb)]
        return remote(src, n_all.at[dev(chip), :, lanes_of(sb)], pag_send.at[sb, i], pag_recv.at[sb, i], partner)

    def ag_first(sb):
        for d in (0, 1):
            ag_ring(sb, d, 0).start()
        ag_partner(sb, z, own=True).start()

    def ag_next(sb, r):
        for d in (0, 1):
            if r <= HOPS[d]:
                ag_ring(sb, d, r - 1).wait_recv()
                if r < HOPS[d]:
                    ag_ring(sb, d, r).start()
                ag_partner(sb, z - sign(sb, d) * r).start()

    def ag_wait(sb):
        def body(i, _):
            ag_partner(sb, i).wait_recv()
            return 0
        lax.fori_loop(0, nz, body, 0)

    def n_loads(b):
        sb, j = b // per_sb, lax.rem(b, per_sb)
        return [pltpu.make_async_copy(n_all.at[j * TILES + a, :, lanes_of(sb)],
                                      nblk.at[lax.rem(b, 4), :, pl.ds(a * LANE, LANE)],
                                      nl_sem.at[lax.rem(b, 4), a]) for a in range(TILES)]

    def dn_moves(b):
        sb, j, sl = b // per_sb, lax.rem(b, per_sb), lax.rem(b, 2)
        out = []
        for h in range(TILES // CORES):
            chip = j * (TILES // CORES) + h
            here = pl.ds(pl.multiple_of((h * CORES + core) * LANE, LANE), LANE)
            there = pl.ds(pl.multiple_of((h * CORES + 1 - core) * LANE, LANE), LANE)
            out.append((pltpu.make_async_copy(dnb.at[sl, :, here], dnp.at[sb, chip], dnp_sem.at[sl, h]),
                        remote(dnb.at[sl, :, there], prx.at[sb, chip], pair_send.at[sl, h],
                               pair_recv.at[sb, chip], partner)))
        return out

    def tile_loads(sb, chip, k):
        chip = lax.rem(chip + 2 * nz, nz)
        return [pltpu.make_async_copy(dnp.at[sb, chip], ownv.at[k, 0], ov_sem.at[k, 0]),
                pltpu.make_async_copy(prx.at[sb, chip], ownv.at[k, 1], ov_sem.at[k, 1])]

    def rx_slot(sb, d, r):
        return rx.at[lax.rem(sb, 2), d * HOPS[0] + r]

    def ring_copy(sb, d, r):
        return remote(sendb.at[d], rx_slot(sb, d, r), ring_send.at[d],
                      ring_recv.at[lax.rem(sb, 2), d * HOPS[0] + r], at(dev(z + sign(sb, d))))

    def ring_target(sb, d, r):
        return z + sign(sb, d) * (HOPS[d] - r)

    def st_pair(b):
        sl = lax.rem(b, 4)
        return remote(own_s.at[sl, 1 - core], x1.at[sl], st_send.at[sl, 0], st_recv.at[sl, 0], partner)

    def st_chip(b, k):
        sl = lax.rem(b, 4)
        return remote(x2.at[sl, z], x2.at[sl, z], st_send.at[sl, k], st_recv.at[sl, nz - k], at(dev(z + k)))

    def st_back(b):
        sl = lax.rem(b, 4)
        return remote(Sb.at[sl, core], Sb.at[sl, core], st_send.at[sl, nz], st_recv.at[sl, nz], partner)

    def lab_copy(k):
        return remote(lab_own, lab_all.at[me], lab_send.at[k - 1], lab_recv.at[n_pp - 1 - k],
                      at(lax.rem(me + k, n_pp)))

    own_copy = pltpu.make_async_copy(n_own, n_all.at[me], io_sem.at[0])
    own_copy.start()
    barrier = pltpu.get_barrier_semaphore()
    for k in range(1, n_pp):
        pl.semaphore_signal(barrier, inc=1, device_id=at(lax.rem(me + k, n_pp)), device_id_type=MESH)
    pl.semaphore_wait(barrier, n_pp - 1)
    ag_first(0)
    for k in range(1, n_pp):
        lab_copy(k).start()
    lab_all[me] = lab_own[...]
    dW[...] = jnp.zeros_like(dW)
    for r in range(1, HOPS[0] + 1):
        ag_next(0, r)
        if r == HOPS[0] - 1 and nsb > 1:
            ag_first(1)
    own_copy.wait()
    ag_wait(0)
    for c in n_loads(0):
        c.start()

    base = me * V

    def forward(b):
        for c in n_loads(b):
            c.wait()
        zl = jnp.dot(W[...], nblk[lax.rem(b, 4)], preferred_element_type=F32)
        t = jnp.tanh(zl * (1.0 / SOFT_CAP))
        U[lax.rem(b, 3)] = t
        s = jnp.sum(jnp.exp2(t * EXP2_SCALE).reshape(V // 8, 8, TB), axis=0)
        s = jnp.sum(s, axis=0, keepdims=True)
        for h in range(CORES):
            own_s[lax.rem(b, 4), h] = s[:, h * HALF:(h + 1) * HALF]
        st_pair(b).start()

    def backward(b):
        sl4 = lax.rem(b, 4)
        st_back(b).wait_recv()
        sb, j = b // per_sb, lax.rem(b, per_sb)
        for h in range(CORES):
            s = Sb[sl4, h]
            s_out[b, :, h * HALF:(h + 1) * HALF] = s
            svec[:, h * HALF:(h + 1) * HALF] = 1.0 / (s * total)
        for a in range(TILES):
            labm[:, a * LANE:(a + 1) * LANE] = lab_all[j * TILES + a, :, lanes_of(sb)] - base
        t = U[lax.rem(b, 3)]
        p = jnp.exp2(t * EXP2_SCALE) * svec[...]
        hit = lax.broadcasted_iota(jnp.int32, (V, TB), 0) == labm[...]
        tl = jnp.sum(jnp.where(hit, t, 0.0).reshape(V // 8, 8, TB), axis=0)
        g = p - jnp.where(hit, 1.0 / total, 0.0)
        dz = (g * (1.0 - t * t)).astype(BF16)
        sl = lax.rem(b, 2)
        dnb[sl, pl.ds(0, D), :] = jnp.dot(WT[...], dz, preferred_element_type=F32)
        dnb[sl, pl.ds(D, PAD_ROWS), :] = tl
        dW[...] += lax.dot_general(nblk[sl4], dz, (((1,), (1,)), ((), ())), preferred_element_type=F32)
        for keep, give in dn_moves(b):
            keep.start()
            give.start()
        st_pair(b).wait_send()
        for k in range(1, nz):
            st_chip(b, k).wait_send()
        st_back(b).wait_send()

    RS0 = per_sb + 3

    def step(s, _):
        @pl.when((s >= 1) & (s - 1 < nb))
        def _():
            b = s - 1
            sl = lax.rem(b, 4)
            st_pair(b).wait_recv()
            x2[sl, z] = own_s[sl, core] + x1[sl]
            for k in range(1, nz):
                st_chip(b, k).start()

        @pl.when((s >= 2) & (s - 2 < nb))
        def _():
            b = s - 2
            sl = lax.rem(b, 4)
            for k in range(1, nz):
                st_chip(b, k).wait_recv()
            acc = x2[sl, 0]
            for k in range(1, nz):
                acc = acc + x2[sl, k]
            Sb[sl, core] = acc
            st_back(b).start()

        for r in range(HOPS[0], 0, -1):
            sb = s + 2 - r

            @pl.when((sb >= 1) & (sb < nsb))
            def _():
                ag_next(sb, r)

        @pl.when(s + 2 < nsb)
        def _():
            ag_first(s + 2)

        @pl.when((lax.rem(s + 1, per_sb) == 0) & (s + 1 < nb))
        def _():
            ag_wait((s + 1) // per_sb)

        @pl.when(s + 1 < nb)
        def _():
            for c in n_loads(s + 1):
                c.start()

        @pl.when((s >= 4) & (s - 4 < nb))
        def _():
            for keep, give in dn_moves(s - 4):
                keep.wait()
                give.wait_send()

        q = s - RS0
        rsb, r = q // per_sb, lax.rem(q, per_sb)

        @pl.when((q >= 0) & (rsb < nsb) & (r == 0))
        def _():
            def body(i, _):
                remote(dnb.at[0, :, pl.ds(0, LANE)], prx.at[rsb, i], pair_send.at[0, 0], pair_recv.at[rsb, i],
                       partner).wait_recv()
                return 0
            lax.fori_loop(0, nz, body, 0)

        @pl.when((q >= 0) & (rsb < nsb))
        def _():
            for d in (0, 1):
                @pl.when(r < HOPS[d])
                def _():
                    for c in tile_loads(rsb, ring_target(rsb, d, r), d):
                        c.start()

        last = (q >= per_sb) & (r == 0)

        @pl.when(last)
        def _():
            for c in tile_loads(rsb - 1, z, 2):
                c.start()

        @pl.when(s < nb)
        def _():
            forward(s)

        @pl.when((q >= 1) & (q - 1 < nsb * per_sb))
        def _():
            for d in (0, 1):
                @pl.when(lax.rem(q - 1, per_sb) < HOPS[d])
                def _():
                    ring_copy((q - 1) // per_sb, d, lax.rem(q - 1, per_sb)).wait_send()

        @pl.when(last)
        def _():
            for c in tile_loads(rsb - 1, z, 2):
                c.wait()
            for d in (0, 1):
                ring_copy(rsb - 1, d, HOPS[d] - 1).wait_recv()

            @pl.when(q >= 2 * per_sb)
            def _():
                pltpu.make_async_copy(outv, dn_out.at[:, lanes_of(rsb - 2)], io_sem.at[1]).wait()
            acc = ownv[2, 0] + ownv[2, 1]
            for d in (0, 1):
                acc = acc + rx[lax.rem(rsb - 1, 2), d * HOPS[0] + HOPS[d] - 1]
            outv[...] = acc
            pltpu.make_async_copy(outv, dn_out.at[:, lanes_of(rsb - 1)], io_sem.at[1]).start()

        @pl.when((q >= 0) & (rsb < nsb))
        def _():
            for d in (0, 1):
                @pl.when(r < HOPS[d])
                def _():
                    for c in tile_loads(rsb, ring_target(rsb, d, r), d):
                        c.wait()

                    @pl.when(r == 0)
                    def _():
                        sendb[d] = ownv[d, 0] + ownv[d, 1]

                    @pl.when(r > 0)
                    def _():
                        ring_copy(rsb, d, r - 1).wait_recv()
                        sendb[d] = ownv[d, 0] + ownv[d, 1] + rx[lax.rem(rsb, 2), d * HOPS[0] + r - 1]
                    ring_copy(rsb, d, r).start()

        @pl.when(s == 2)
        def _():
            for k in range(1, n_pp):
                lab_copy(k).wait_recv()

        @pl.when((s >= 2) & (s - 2 < nb))
        def _():
            backward(s - 2)
        return 0
    lax.fori_loop(0, RS0 + nsb * per_sb + 1, step, 0)

    pltpu.make_async_copy(outv, dn_out.at[:, lanes_of(nsb - 1)], io_sem.at[1]).wait()
    w_store = pltpu.make_async_copy(dW, dW_out, io_sem.at[0])
    w_store.start()
    for k in range(1, n_pp):
        lab_copy(k).wait_send()

    def finish(sb, _):
        for d in (0, 1):
            for r in range(HOPS[d]):
                ag_ring(sb, d, r).wait_send()

        def body(i, _):
            ag_partner(sb, i).wait_send()
            return 0
        lax.fori_loop(0, nz, body, 0)
        return 0
    lax.fori_loop(0, nsb, finish, 0)
    w_store.wait()


def mega_call(n_own, lab_own, W, WT, *, n_pp, total, cid=1):
    D, T = n_own.shape
    V = W.shape[0]
    D8, nz, nsb = D + PAD_ROWS, n_pp // CORES, T // LANE
    nb = nsb * n_pp // TILES
    hbm, vmem = pl.BlockSpec(memory_space=pl.ANY), pl.BlockSpec(memory_space=pltpu.VMEM)
    dma, sd = pltpu.SemaphoreType.DMA, jax.ShapeDtypeStruct
    out = pl.pallas_call(
        functools.partial(kernel, n_pp, float(total)),
        out_shape=[sd((D8, T), F32), sd((D, V), F32), sd((nb, 1, TB), F32),
                   sd((n_pp, D, T), BF16), sd((nsb, nz, D8, LANE), F32), sd((nsb, nz, D8, LANE), F32)],
        in_specs=[vmem] * 4,
        out_specs=[hbm, hbm, vmem, hbm, hbm, hbm],
        scratch_shapes=[
            pltpu.VMEM((3, V, TB), F32), pltpu.VMEM((4, D, TB), BF16), pltpu.VMEM((D, V), F32),
            pltpu.VMEM((2, D8, TB), F32), pltpu.VMEM((1, TB), F32), pltpu.VMEM((1, TB), jnp.int32),
            pltpu.VMEM((n_pp, 1, T), jnp.int32), pltpu.VMEM((4, CORES, 1, HALF), F32), pltpu.VMEM((4, 1, HALF), F32),
            pltpu.VMEM((4, nz, 1, HALF), F32), pltpu.VMEM((4, CORES, 1, HALF), F32),
            pltpu.VMEM((2, sum(HOPS), D8, LANE), F32), pltpu.VMEM((3, 2, D8, LANE), F32),
            pltpu.VMEM((2, D8, LANE), F32), pltpu.VMEM((D8, LANE), F32),
            dma((nsb, 2, HOPS[0])), dma((nsb, 2, HOPS[0])), dma((nsb, nz)), dma((nsb, nz)),
            dma((nsb, nz)), dma((2, 2)), dma((2, 2)), dma((2, sum(HOPS))), dma((2,)),
            dma((4, nz + 1)), dma((4, nz + 1)), dma((n_pp - 1,)), dma((n_pp - 1,)), dma((4, TILES)), dma((3, 2)), dma((2,)),
        ],
        compiler_params=pltpu.CompilerParams(vmem_limit_bytes=63 * 1024 * 1024, collective_id=cid, has_side_effects=True),
        cost_estimate=pl.CostEstimate(flops=6 * n_pp * T * D * V, bytes_accessed=n_pp * T * D * 20, transcendentals=0),
        name="head")(n_own, lab_own, W, WT)
    return out[:3]


def sum_kernel(n_pp, x_ref, o_ref, rbuf, send_sem, recv_sem):
    me = lax.axis_index("pp")

    def peer(k):
        return {"pp": lax.rem(me + k, n_pp)}

    barrier = pltpu.get_barrier_semaphore()
    for k in range(1, n_pp):
        pl.semaphore_signal(barrier, inc=1, device_id=peer(k), device_id_type=MESH)
    pl.semaphore_wait(barrier, n_pp - 1)
    copies = [pltpu.make_async_remote_copy(
        src_ref=x_ref, dst_ref=rbuf.at[me], send_sem=send_sem.at[k - 1], recv_sem=recv_sem.at[n_pp - 1 - k],
        device_id=peer(k), device_id_type=MESH) for k in range(1, n_pp)]
    for c in copies:
        c.start()
    for c in copies:
        c.wait_recv()
    acc = jnp.zeros_like(o_ref)
    for k in range(n_pp):
        acc = acc + jnp.where(k == me, x_ref[...], rbuf[k])
    o_ref[...] = acc
    for c in copies:
        c.wait_send()


def small_sum(x, n_pp, cid):
    vmem = pl.BlockSpec(memory_space=pltpu.VMEM)
    return pl.pallas_call(
        functools.partial(sum_kernel, n_pp), out_shape=jax.ShapeDtypeStruct(x.shape, F32),
        in_specs=[vmem], out_specs=vmem,
        scratch_shapes=[pltpu.VMEM((n_pp,) + x.shape, F32), pltpu.SemaphoreType.DMA((n_pp - 1,)),
                        pltpu.SemaphoreType.DMA((n_pp - 1,))],
        compiler_params=pltpu.CompilerParams(collective_id=cid, has_side_effects=True), name="small_sum")(x)


def norm_cols(cols, gain):
    mean_sq = jnp.mean(cols * cols, axis=1, keepdims=True)
    return cols * lax.rsqrt(mean_sq + EPS) * (1.0 + gain)[None, :, None]


def solution(mesh):
    n_pp = mesh.shape["pp"]

    def local_fn(hidden, labels, gamma, table):
        mb, seq, D = hidden.shape
        V = table.shape[0]
        T = mb * seq
        total = T * n_pp
        me = lax.axis_index("pp")
        cols = jnp.swapaxes(hidden, 1, 2).astype(F32)
        normed, norm_vjp = jax.vjp(norm_cols, cols, gamma)
        normed = jnp.concatenate(list(normed.astype(BF16)), axis=1)
        dn, dW, s = mega_call(normed, labels.reshape(1, T), table, table.T, n_pp=n_pp, total=total)
        s = lax.dynamic_index_in_dim(s.reshape(T // LANE, n_pp, LANE), me, 1, keepdims=False).reshape(T)
        loss = jnp.log(s) - SOFT_CAP * jnp.sum(dn[D:], axis=0)
        d_cols, d_gain = norm_vjp(dn[:D].reshape(D, mb, seq).swapaxes(0, 1))
        flat = jnp.concatenate([d_gain, jnp.sum(loss)[None]])
        rows = -(-flat.shape[0] // 1024) * 8
        flat = jnp.pad(flat, (0, rows * 128 - flat.shape[0])).reshape(rows, 128)
        flat = small_sum(flat, n_pp, 2).reshape(-1)
        return (loss.reshape(mb, seq), jnp.swapaxes(d_cols, 1, 2).astype(BF16), flat[D:D + 1] / total,
                dW.T, flat[:D])

    token_spec = P(("dp", "pp"))
    return jax.shard_map(local_fn, mesh=mesh,
                         in_specs=(token_spec, token_spec, P(), P("pp")),
                         out_specs=(token_spec, token_spec, P("dp"), token_spec, P("dp")),
                         check_vma=False)
```

time: 2880 us -> 444 us (0.15)
  blocking collectives: 1560 us -> 0 us
  matrix products: 823 us -> 0 us
  Pallas kernels: 0 us -> 408 us
  waiting for transfers between devices: 284 us -> 0 us
  other arithmetic: 187 us -> 13.5 us
    dot_general x96 -> x0, matrix products: 823 us -> none  [the longest x32 392 us: micro_step(): lax.dot_general(grad_logits, block, (((0,), (0,)), ((), ())), preferred_e...]
    psum x33 -> x0, blocking collectives: 782 us -> none  [the longest x32 757 us: micro_step(): group_stats = lax.psum(local_stats, 'pp')]
    pmax x32 -> x0, blocking collectives: 755 us -> none  [micro_step(): row_max = lax.pmax(jnp.max(capped, axis=1), 'pp')]
    pallas_call x0 -> x2, Pallas kernels: none -> 408 us  [the longest x1 394 us: mega_call(): pl.pallas_call(functools.partial(kernel, n_pp, float(total)), out_shape=[...]
    reduce_scatter x1 -> x0, waiting for transfers between devices: 200 us -> none  [local_fn(): own_dn = lax.psum_scatter(all_dn, 'pp', scatter_dimension=0, tiled=True)]
    reduce_sum x35 -> x4, other arithmetic: 179 us -> 5.16 us  [the longest x1 1.53 us: norm_cols(): mean_sq = jnp.mean(cols * cols, axis=1, keepdims=True)]
    all_gather x1 -> x0, waiting for transfers between devices: 84 us -> none  [local_fn(): all_normed = lax.all_gather(normed, 'pp', axis=0, tiled=True)]
  transfers between devices with their start and end apart: 2 -> 0, of which waited for: 2 -> 0; matrix products, arithmetic and copies ran while one was open for 0% -> 0% of each run, Pallas kernels for 0% -> 0%
where the time goes in v2:
time: 444 us; the launch traced here: 443 us
  Pallas kernels  408 us (92%)
  local copies, waits for them, and re-layouts  18.6 us (4%)
  other arithmetic  13.5 us (3%)
    pallas_call x1, Pallas kernels, mega_call(): pl.pallas_call(functools.partial(kernel, n_pp, float(total)), out_shape=[...  394 us
    pallas_call x1, Pallas kernels, small_sum(): pl.pallas_call(functools.partial(sum_kernel, n_pp), out_shape=jax.ShapeDt...  13.9 us
    unnamed x24, local copies, waits for them, and re-layouts  13.5 us

profile of v2, /device:TPU:21, one launch (start us, length us, event | category | flops | bytes accessed | tf_op | source)
XLA Modules:
  0.0 443.0 jit_solution(16641807959437414351)
XLA Ops:
  0.6 1.5 fusion.7
  2.2 0.0 copy-start.6
  2.2 0.6 copy-done.6
  2.7 0.0 copy-start.2
  2.7 0.7 broadcast_add_fusion
  3.4 0.0 copy-start.4
  3.4 1.6 fusion.5
  5.0 0.0 copy-start.1
  5.0 0.1 slice_bitcast_fusion.1
  5.1 0.0 copy-done.2
  5.1 0.0 copy-done.4
  5.1 1.2 pad_maximum_fusion.n_own
  6.3 1.2 copy-done.1
  7.5 0.0 copy-start.9
  7.5 3.7 copy.10.W
  11.1 0.0 copy-done.9
  11.1 0.6 copy.14
  11.7 394.4 %head.1 = (f32[584,1024]{1,0:T(8,128)}, f32[576,3072]{1,0:T(8,128)}, f32[32,1,512]{2,1,0:T(1,128)}, bf16[16,576,1024]{2,1,0:T(8,128)(2,1)}, f32[8,8,584,128]{3,2,1,0:T(8,128)}, /*index=5*/f32[8,8,584,128]{3,2,1,0:T(8,128)}) custom-call(bf16[576,1024]{1,0:T(8,128)(2,1)} %pad_maximum_fusion.n_own, s32[1,1024]{1,0:T(1,128)} %bitcast.72, ...), custom_call_target="tpu_custom_call" | custom-call | flops 173946175488 | bytes 188743680 | tf_op jit(solution)/shard_map/head/pallas_call | solution.py:362
  406.2 0.8 slice_reduce_fusion
  407.0 1.5 subtract_reduce_fusion
  408.4 0.0 copy-start
  408.4 0.0 copy-start.3
  408.4 0.0 copy-start.5
  408.4 1.9 slice.13
  410.4 0.0 copy-start.7
  410.4 0.0 copy-done
  410.4 0.0 copy-done.3
  410.4 0.0 copy-done.5
  410.4 1.4 fusion.6
  411.8 1.3 fusion.13.x_ref
  413.1 13.9 %small_sum.1 = f32[8,128]{1,0:T(8,128)} custom-call(f32[8,128]{1,0:T(8,128)} %fusion.13.x_ref), custom_call_target="tpu_custom_call" | custom-call | tf_op jit(solution)/shard_map/small_sum/pallas_call | solution.py:412
  427.1 1.3 slice.14
  429.0 1.3 log.9
  430.2 0.6 mul.96
  430.8 1.3 sub.7
  432.1 0.0 copy-done.7
  432.1 0.7 multiply_multiply_fusion
  432.9 1.6 fusion.9
  434.4 0.0 copy-start.8
  434.4 6.8 %copy.20 = f32[3072,576]{0,1:T(8,128)} copy(f32[3072,576]{0,1:T(8,128)} %bitcast.66) | data formatting | bytes 14155776
  441.2 0.0 copy-done.8
  441.2 0.6 copy.21
  (2 shorter events, 0.0 us)
Async XLA Ops:
  2.2 0.6 copy-start.6
  2.7 2.4 copy-start.2
  3.4 1.7 copy-start.4
  5.0 2.4 copy-start.1
  7.5 3.7 copy-start.9
  408.4 2.0 copy-start
  408.4 2.0 copy-start.3
  408.4 2.0 copy-start.5
  410.4 21.8 %copy-start.7 = (f32[2,512]{1,0:T(2,128)S(1)}, f32[2,512]{1,0:T(2,128)}, u32[]{:S(2)}) copy-start(f32[2,512]{1,0:T(2,128)} %copy-done.6) | copy-start | bytes 12292
  434.4 6.8 %copy-start.8 = (f32[8,128]{1,0:T(8,128)S(1)}, f32[8,128]{1,0:T(8,128)}, u32[]{:S(2)}) copy-start(f32[8,128]{1,0:T(8,128)} %small_sum.1) | copy-start | bytes 12292

commit v3 on v2

v3 whole, which is shorter than its diff:
```python
import functools
import math

import jax
import jax.numpy as jnp
from jax import lax
from jax.experimental import pallas as pl
from jax.experimental.pallas import tpu as pltpu
from jax.sharding import PartitionSpec as P

F32, BF16 = jnp.float32, jnp.bfloat16
SOFT_CAP = 30.0
EPS = 1e-6
EXP2_SCALE = SOFT_CAP * math.log2(math.e)
MESH = pl.DeviceIdType.MESH
CORES = 2
LANE = 128
TILES = 4
TB = LANE * TILES
HALF = TB // CORES
PAD_ROWS = 8
PIECES = 4
WROWS = 256
HOPS = (4, 3)


def kernel(n_pp, total, hid, lab_own, gamma, WT,
           dh, dW, loss_out, ex_out, n_all, dnp, prx,
           n_own, W, gain, rinv, dgacc, lacc, s_out, ex_own, ex_rx,
           U, nblk, dnb, svec, labm, lab_all, own_s, x1, x2, Sb, rx, ownv, sendb,
           ag_recv, ag_send, pag_recv, pag_send, pair_recv, pair_send, dnp_sem, ring_recv, ring_send,
           st_recv, st_send, lab_recv, lab_send, nl_sem, ov_sem, io_sem, tail_recv, tail_send, tl_sem, ex_recv, ex_send,
           first_recv, first_send, firstp_recv, firstp_send):
    D, T = n_own.shape
    V = W.shape[0]
    seq = hid.shape[2]
    per_mb = seq // LANE
    wrows = min(WROWS, V)
    D8 = D + PAD_ROWS
    nz = n_pp // CORES
    nsb = T // LANE
    per_sb = n_pp // TILES
    nb = nsb * per_sb
    me = lax.axis_index("pp")
    z, core = me // CORES, lax.rem(me, CORES)

    def dev(chip, c=core):
        return lax.rem(chip + 2 * nz, nz) * CORES + c

    def at(index):
        return {"pp": index}

    partner = at(z * CORES + 1 - core)

    def lanes_of(sb):
        return pl.ds(pl.multiple_of(sb * LANE, LANE), LANE)

    def remote(src, dst, ssem, rsem, where):
        return pltpu.make_async_remote_copy(src_ref=src, dst_ref=dst, send_sem=ssem, recv_sem=rsem,
                                            device_id=where, device_id_type=MESH)

    def mb_lanes(sb):
        return pl.ds(pl.multiple_of(lax.rem(sb, per_mb) * LANE, LANE), LANE)

    def sign(sb, d):
        g = 1 - 2 * lax.rem(sb, 2)
        return g if d == 0 else -g

    def ag_ring(sb, d, r):
        g = sign(sb, d)
        if r == 0:
            src = n_own.at[:, lanes_of(sb)]
        else:
            src = n_all.at[dev(z - g * r), :, lanes_of(sb)]
        return remote(src, n_all.at[dev(z - g * r), :, lanes_of(sb)], ag_send.at[sb, d, r], ag_recv.at[sb, d, r],
                      at(dev(z + g)))

    def ag_partner(sb, chip, own=False):
        i = lax.rem(chip + 2 * nz, nz)
        src = n_own.at[:, lanes_of(sb)] if own else n_all.at[dev(chip), :, lanes_of(sb)]
        return remote(src, n_all.at[dev(chip), :, lanes_of(sb)], pag_send.at[sb, i], pag_recv.at[sb, i], partner)

    rows0 = D // PIECES

    def first_ring(d, r, p):
        g = sign(0, d)
        rows = pl.ds(p * rows0, rows0)
        src = n_own.at[rows, pl.ds(0, LANE)] if r == 0 else n_all.at[dev(z - g * r), rows, pl.ds(0, LANE)]
        return remote(src, n_all.at[dev(z - g * r), rows, pl.ds(0, LANE)], first_send.at[d, r, p],
                      first_recv.at[d, r, p], at(dev(z + g)))

    def first_partner(d, r, p):
        g = sign(0, d)
        rows = pl.ds(p * rows0, rows0)
        src = n_own.at[rows, pl.ds(0, LANE)] if r == 0 else n_all.at[dev(z - g * r), rows, pl.ds(0, LANE)]
        return remote(src, n_all.at[dev(z - g * r), rows, pl.ds(0, LANE)], firstp_send.at[d, r, p],
                      firstp_recv.at[d, r, p], partner)

    FIRSTP = [(d, r) for r in range(HOPS[0] + 1) for d in (0, 1) if r <= HOPS[d] and (r, d) != (0, 1)]

    def ag_first(sb):
        for d in (0, 1):
            ag_ring(sb, d, 0).start()
        ag_partner(sb, z, own=True).start()

    def ag_next(sb, r):
        for d in (0, 1):
            if r <= HOPS[d]:
                ag_ring(sb, d, r - 1).wait_recv()
                if r < HOPS[d]:
                    ag_ring(sb, d, r).start()
                ag_partner(sb, z - sign(sb, d) * r).start()

    def ag_wait(sb):
        def body(i, _):
            ag_partner(sb, i).wait_recv()
            return 0
        lax.fori_loop(0, nz, body, 0)

    def n_loads(b):
        sb, j = b // per_sb, lax.rem(b, per_sb)
        return [pltpu.make_async_copy(n_all.at[j * TILES + a, :, lanes_of(sb)],
                                      nblk.at[lax.rem(b, 4), :, pl.ds(a * LANE, LANE)],
                                      nl_sem.at[lax.rem(b, 4), a]) for a in range(TILES)]

    def dn_moves(b):
        sb, j, sl = b // per_sb, lax.rem(b, per_sb), lax.rem(b, 2)
        out = []
        for h in range(TILES // CORES):
            chip = j * (TILES // CORES) + h
            here = pl.ds(pl.multiple_of((h * CORES + core) * LANE, LANE), LANE)
            there = pl.ds(pl.multiple_of((h * CORES + 1 - core) * LANE, LANE), LANE)
            out.append((pltpu.make_async_copy(dnb.at[sl, :, here], dnp.at[sb, chip], dnp_sem.at[sl, h]),
                        remote(dnb.at[sl, :, there], prx.at[sb, chip], pair_send.at[sl, h],
                               pair_recv.at[sb, chip], partner)))
        return out

    def tile_loads(sb, chip, k):
        chip = lax.rem(chip + 2 * nz, nz)
        return [pltpu.make_async_copy(dnp.at[sb, chip], ownv.at[k, 0], ov_sem.at[k, 0]),
                pltpu.make_async_copy(prx.at[sb, chip], ownv.at[k, 1], ov_sem.at[k, 1])]

    def rx_slot(sb, d, r):
        return rx.at[lax.rem(sb, 2), d * HOPS[0] + r]

    cut = D8 // 16 * 8
    part = (pl.ds(0, cut), pl.ds(cut, D8 - cut))

    def ring_copy(sb, d, r, h):
        return remote(sendb.at[d, part[h]], rx_slot(sb, d, r).at[part[h]], ring_send.at[d, h],
                      ring_recv.at[lax.rem(sb, 2), d * HOPS[0] + r, h], at(dev(z + sign(sb, d))))

    def ring_step(q, h):
        sb, r = q // per_sb, lax.rem(q, per_sb)
        for d in (0, 1):
            @pl.when((q >= 1) & (q - 1 < n_rs * per_sb) & (lax.rem(q - 1, per_sb) < HOPS[d]))
            def _():
                ring_copy((q - 1) // per_sb, d, lax.rem(q - 1, per_sb), h).wait_send()

            @pl.when((q >= 0) & (sb < n_rs) & (r < HOPS[d]))
            def _():
                if h == 0:
                    for c in tile_loads(sb, ring_target(sb, d, r), d):
                        c.wait()

                @pl.when(r == 0)
                def _():
                    sendb[d, part[h], :] = ownv[d, 0, part[h], :] + ownv[d, 1, part[h], :]

                @pl.when(r > 0)
                def _():
                    ring_copy(sb, d, r - 1, h).wait_recv()
                    sendb[d, part[h], :] = (ownv[d, 0, part[h], :] + ownv[d, 1, part[h], :]
                                            + rx[lax.rem(sb, 2), d * HOPS[0] + r - 1, part[h], :])
                ring_copy(sb, d, r, h).start()

    def own_tile(sb):
        for c in tile_loads(sb, z, 2):
            c.wait()
        for d in (0, 1):
            for h in (0, 1):
                ring_copy(sb, d, HOPS[d] - 1, h).wait_recv()
        acc = ownv[2, 0] + ownv[2, 1]
        for d in (0, 1):
            acc = acc + rx[lax.rem(sb, 2), d * HOPS[0] + HOPS[d] - 1]
        finish_tile(sb, acc)

    def ring_target(sb, d, r):
        return z + sign(sb, d) * (HOPS[d] - r)

    def st_pair(b):
        sl = lax.rem(b, 4)
        return remote(own_s.at[sl, 1 - core], x1.at[sl], st_send.at[sl, 0], st_recv.at[sl, 0], partner)

    def st_chip(b, k):
        sl = lax.rem(b, 4)
        return remote(x2.at[sl, z], x2.at[sl, z], st_send.at[sl, k], st_recv.at[sl, nz - k], at(dev(z + k)))

    def st_back(b):
        sl = lax.rem(b, 4)
        return remote(Sb.at[sl, core], Sb.at[sl, core], st_send.at[sl, nz], st_recv.at[sl, nz], partner)

    def lab_copy(k):
        return remote(lab_own, lab_all.at[me], lab_send.at[k - 1], lab_recv.at[n_pp - 1 - k],
                      at(lax.rem(me + k, n_pp)))

    def hid_tile(sb):
        return hid[sb // per_mb, :, mb_lanes(sb)].astype(F32)

    def norm_tile(sb):
        h = hid_tile(sb)
        r = lax.rsqrt(jnp.mean(h * h, axis=0, keepdims=True) + EPS)
        rinv[sb] = r
        n_own[:, lanes_of(sb)] = (h * r * gain[...]).astype(BF16)

    def turn_table(c):
        rows = pl.ds(pl.multiple_of(c * wrows, wrows), wrows)
        W[rows, :] = WT[:, rows].T

    gain[...] = jnp.broadcast_to(1.0 + gamma[...], (LANE, D)).T
    norm_tile(0)
    barrier = pltpu.get_barrier_semaphore()
    for k in range(1, n_pp):
        pl.semaphore_signal(barrier, inc=1, device_id=at(lax.rem(me + k, n_pp)), device_id_type=MESH)
    pl.semaphore_wait(barrier, n_pp - 1)
    for p in range(PIECES):
        for d in (0, 1):
            first_ring(d, 0, p).start()
        first_partner(0, 0, p).start()
    for k in range(1, n_pp):
        lab_copy(k).start()
    lab_all[me] = lab_own[...]

    def rest(sb, _):
        norm_tile(sb)
        return 0
    lax.fori_loop(1, nsb, rest, 0)
    own_copy = pltpu.make_async_copy(n_own, n_all.at[me], io_sem.at[0])
    own_copy.start()
    dW[...] = jnp.zeros_like(dW)
    dgacc[...] = jnp.zeros_like(dgacc)
    lacc[...] = jnp.zeros_like(lacc)
    n_turn = V // wrows
    for r in range(1, HOPS[0] + 1):
        def turn(c, _):
            turn_table(c)
            return 0
        lax.fori_loop(n_turn * (r - 1) // HOPS[0], n_turn * r // HOPS[0], turn, 0)
        for p in range(PIECES):
            for d in (0, 1):
                if r <= HOPS[d]:
                    first_ring(d, r - 1, p).wait_recv()
                    if r < HOPS[d]:
                        first_ring(d, r, p).start()
                    first_partner(d, r, p).start()
        if r == HOPS[0] - 1 and nsb > 1:
            ag_first(1)
    own_copy.wait()
    for d, r in FIRSTP:
        for p in range(PIECES):
            first_partner(d, r, p).wait_recv()
    for c in n_loads(0):
        c.start()

    base = me * V

    def forward(b):
        for c in n_loads(b):
            c.wait()
        zl = jnp.dot(W[...], nblk[lax.rem(b, 4)], preferred_element_type=F32)
        t = jnp.tanh(zl * (1.0 / SOFT_CAP))
        U[lax.rem(b, 3), pl.ds(0, V), :] = t
        s = jnp.sum(jnp.exp2(t * EXP2_SCALE).reshape(V // 8, 8, TB), axis=0)
        s = jnp.sum(s, axis=0, keepdims=True)
        for h in range(CORES):
            own_s[lax.rem(b, 4), h] = s[:, h * HALF:(h + 1) * HALF]
        st_pair(b).start()

    def backward(b):
        sl4 = lax.rem(b, 4)
        st_back(b).wait_recv()
        sb, j = b // per_sb, lax.rem(b, per_sb)
        for h in range(CORES):
            s = Sb[sl4, h]
            s_out[b, :, h * HALF:(h + 1) * HALF] = s
            svec[:, h * HALF:(h + 1) * HALF] = 1.0 / (s * total)
        for a in range(TILES):
            rows = lab_all[j * TILES + a, :, mb_lanes(sb)]
            row = rows[0:1]
            for m in range(1, rows.shape[0]):
                row = jnp.where(sb // per_mb == m, rows[m:m + 1], row)
            labm[:, a * LANE:(a + 1) * LANE] = row - base
        t = U[lax.rem(b, 3), pl.ds(0, V), :]
        p = jnp.exp2(t * EXP2_SCALE) * svec[...]
        hit = lax.broadcasted_iota(jnp.int32, (V, TB), 0) == labm[...]
        tl = jnp.sum(jnp.where(hit, t, 0.0).reshape(V // 8, 8, TB), axis=0)
        g = p - jnp.where(hit, 1.0 / total, 0.0)
        dz = (g * (1.0 - t * t)).astype(BF16)
        sl = lax.rem(b, 2)
        dnb[sl, pl.ds(0, D), :] = jnp.dot(WT[...], dz, preferred_element_type=F32)
        dnb[sl, pl.ds(D, PAD_ROWS), :] = tl
        dW[...] += lax.dot_general(nblk[sl4], dz, (((1,), (1,)), ((), ())), preferred_element_type=F32)
        for keep, give in dn_moves(b):
            keep.start()
            give.start()
        st_pair(b).wait_send()
        for k in range(1, nz):
            st_chip(b, k).wait_send()
        st_back(b).wait_send()

    def finish_tile(sb, acc):
        dn = acc[0:D]
        h = hid_tile(sb)
        r = rinv[sb]
        xhat = h * r
        dgacc[...] += dn * xhat
        dx = dn * gain[...]
        m = jnp.mean(dx * xhat, axis=0, keepdims=True)
        dh[sb // per_mb, :, mb_lanes(sb)] = (
            r * (dx - xhat * m)).astype(BF16)
        own_s = s_out[sb * per_sb + me // TILES, :, pl.ds(pl.multiple_of(lax.rem(me, TILES) * LANE, LANE), LANE)]
        loss = jnp.log(own_s) - SOFT_CAP * jnp.sum(acc[D:D8], axis=0, keepdims=True)
        for m in range(hid.shape[0]):
            @pl.when(sb // per_mb == m)
            def _():
                loss_out[m:m + 1, mb_lanes(sb)] = loss
        lacc[...] += loss

    RS0 = per_sb + 3
    n_rs = nsb - 1

    def step(s, _):
        @pl.when((s >= 1) & (s - 1 < nb))
        def _():
            b = s - 1
            sl = lax.rem(b, 4)
            st_pair(b).wait_recv()
            x2[sl, z] = own_s[sl, core] + x1[sl]
            for k in range(1, nz):
                st_chip(b, k).start()

        @pl.when((s >= 2) & (s - 2 < nb))
        def _():
            b = s - 2
            sl = lax.rem(b, 4)
            for k in range(1, nz):
                st_chip(b, k).wait_recv()
            acc = x2[sl, 0]
            for k in range(1, nz):
                acc = acc + x2[sl, k]
            Sb[sl, core] = acc
            st_back(b).start()

        for r in range(HOPS[0], -1, -1):
            u = s - r
            sb = jnp.where(u <= 1, u + 2, jnp.where(u <= 5, u + 1, 7 + (u - 12) // 4))
            now = ((u >= -1) & (u <= 1)) | ((u >= 3) & (u <= 5)) | ((u >= 12) & (lax.rem(u, 4) == 0))

            @pl.when(now & (sb >= 1) & (sb < nsb))
            def _():
                if r == 0:
                    ag_first(sb)
                else:
                    ag_next(sb, r)

        @pl.when((lax.rem(s + 1, per_sb) == 0) & (s + 1 < nb))
        def _():
            ag_wait((s + 1) // per_sb)

        @pl.when(s + 1 < nb)
        def _():
            for c in n_loads(s + 1):
                c.start()

        @pl.when((s >= 4) & (s - 4 < nb))
        def _():
            for keep, give in dn_moves(s - 4):
                keep.wait()
                give.wait_send()

        q = s - RS0
        rsb, r = q // per_sb, lax.rem(q, per_sb)

        @pl.when((q >= 0) & (rsb < n_rs) & (r == 0))
        def _():
            def body(i, _):
                remote(dnb.at[0, :, pl.ds(0, LANE)], prx.at[rsb, i], pair_send.at[0, 0], pair_recv.at[rsb, i],
                       partner).wait_recv()
                return 0
            lax.fori_loop(0, nz, body, 0)

        @pl.when((q >= 0) & (rsb < n_rs))
        def _():
            for d in (0, 1):
                @pl.when(r < HOPS[d])
                def _():
                    for c in tile_loads(rsb, ring_target(rsb, d, r), d):
                        c.start()

        last = (q >= per_sb) & (r == 0) & (rsb <= n_rs)

        @pl.when(last)
        def _():
            for c in tile_loads(rsb - 1, z, 2):
                c.start()

        @pl.when(s < nb)
        def _():
            forward(s)

        ring_step(q, 0)

        @pl.when(s == 2)
        def _():
            for k in range(1, n_pp):
                lab_copy(k).wait_recv()

        @pl.when((s >= 2) & (s - 2 < nb))
        def _():
            backward(s - 2)

        ring_step(q, 1)

        @pl.when(last)
        def _():
            own_tile(rsb - 1)
        return 0
    n_steps = RS0 + n_rs * per_sb
    lax.fori_loop(0, n_steps, step, 0)

    sb = nsb - 1
    par = sb % 2
    for b in range(max(n_steps - 4, 0), nb):
        for keep, give in dn_moves(b):
            keep.wait()
            give.wait_send()

    def prx_wait(i, _):
        remote(dnb.at[0, :, pl.ds(0, LANE)], prx.at[sb, i], pair_send.at[0, 0], pair_recv.at[sb, i],
               partner).wait_recv()
        return 0
    lax.fori_loop(0, nz, prx_wait, 0)

    def slot(half, e):
        return U.at[half, pl.ds(e // 4 * D8, D8), pl.ds(e % 4 * LANE, LANE)]

    hops = [(d, r) for r in range(HOPS[0]) for d in (0, 1) if r < HOPS[d]]
    loads = []
    for e, chip in enumerate([ring_target(sb, d, r) for d, r in hops] + [z]):
        chip = lax.rem(chip + 2 * nz, nz)
        loads.append([pltpu.make_async_copy(dnp.at[sb, chip], slot(0, e), tl_sem.at[0, e]),
                      pltpu.make_async_copy(prx.at[sb, chip], slot(1, e), tl_sem.at[1, e])])
        for c in loads[-1]:
            c.start()
    cuts = [D8 // 8 * p // PIECES * 8 for p in range(PIECES + 1)]

    def piece(p):
        return pl.ds(cuts[p], cuts[p + 1] - cuts[p])

    def tail_copy(e, p):
        d, r = hops[e]
        return remote(slot(0, e).at[piece(p)], rx.at[par, d * HOPS[0] + r, piece(p)],
                      tail_send.at[e, p], tail_recv.at[d * HOPS[0] + r, p], at(dev(z + sign(sb, d))))

    def tail_arrived(d, r, p):
        remote(slot(0, 0).at[piece(p)], rx.at[par, d * HOPS[0] + r, piece(p)], tail_send.at[0, p],
               tail_recv.at[d * HOPS[0] + r, p], partner).wait_recv()

    if n_rs > 0:
        for c in tile_loads(n_rs - 1, z, 2):
            c.start()
    for e, (d, r) in enumerate(hops):
        if r == 1 and d == 0 and n_rs > 0:
            for h in (0, 1):
                ring_step(jnp.int32(n_rs * per_sb), h)
            own_tile(n_rs - 1)
        for c in loads[e]:
            c.wait()
        for p in range(PIECES):
            mine, other = slot(0, e).at[piece(p)], slot(1, e).at[piece(p)]
            if r > 0:
                tail_arrived(d, r - 1, p)
                mine[...] = mine[...] + other[...] + rx[par, d * HOPS[0] + r - 1, piece(p)]
            else:
                mine[...] = mine[...] + other[...]
            tail_copy(e, p).start()
    for c in loads[len(hops)]:
        c.wait()
    for d in (0, 1):
        for p in range(PIECES):
            tail_arrived(d, HOPS[d] - 1, p)
    finish_tile(sb, slot(0, len(hops))[...] + slot(1, len(hops))[...] + rx[par, HOPS[0] - 1]
                + rx[par, HOPS[0] + HOPS[1] - 1])

    ex_own[:, 0:D] = jnp.sum(dgacc[...].T, axis=0, keepdims=True)
    ex_own[:, pl.ds(ex_own.shape[1] - LANE, LANE)] = lacc[...]
    exs = [remote(ex_own, ex_rx.at[me], ex_send.at[k - 1], ex_recv.at[n_pp - 1 - k], at(lax.rem(me + k, n_pp)))
           for k in range(1, n_pp)]
    for c in exs:
        c.start()
    for c in exs:
        c.wait_recv()
    acc = jnp.zeros_like(ex_out)
    for k in range(n_pp):
        acc = acc + jnp.where(k == me, ex_own[...], ex_rx[k])
    ex_out[...] = acc
    for c in exs:
        c.wait_send()
    for e in range(len(hops)):
        for p in range(PIECES):
            tail_copy(e, p).wait_send()
    for k in range(1, n_pp):
        lab_copy(k).wait_send()

    for p in range(PIECES):
        for d in (0, 1):
            for r in range(HOPS[d]):
                first_ring(d, r, p).wait_send()
        for d, r in FIRSTP:
            first_partner(d, r, p).wait_send()

    def finish(sb, _):
        for d in (0, 1):
            for r in range(HOPS[d]):
                ag_ring(sb, d, r).wait_send()

        def body(i, _):
            ag_partner(sb, i).wait_send()
            return 0
        lax.fori_loop(0, nz, body, 0)
        return 0
    lax.fori_loop(1, nsb, finish, 0)


def mega_call(hid, lab_own, gamma, WT, *, n_pp, total, cid=1):
    mb, D, seq = hid.shape
    T = mb * seq
    V = WT.shape[1]
    D8, nz, nsb = D + PAD_ROWS, n_pp // CORES, T // LANE
    nb = nsb * n_pp // TILES
    EX = -(-D // LANE) * LANE + LANE
    hbm, vmem = pl.BlockSpec(memory_space=pl.ANY), pl.BlockSpec(memory_space=pltpu.VMEM)
    dma, sd = pltpu.SemaphoreType.DMA, jax.ShapeDtypeStruct
    out = pl.pallas_call(
        functools.partial(kernel, n_pp, float(total)),
        out_shape=[sd((mb, D, seq), BF16), sd((D, V), F32), sd((mb, seq), F32), sd((1, EX), F32),
                   sd((n_pp, D, T), BF16), sd((nsb, nz, D8, LANE), F32), sd((nsb, nz, D8, LANE), F32)],
        in_specs=[vmem] * 4,
        out_specs=[vmem, vmem, vmem, vmem, hbm, hbm, hbm],
        scratch_shapes=[
            pltpu.VMEM((D, T), BF16), pltpu.VMEM((V, D), BF16), pltpu.VMEM((D, LANE), F32), pltpu.VMEM((nsb, 1, LANE), F32),
            pltpu.VMEM((D, LANE), F32), pltpu.VMEM((1, LANE), F32), pltpu.VMEM((nb, 1, TB), F32),
            pltpu.VMEM((1, EX), F32), pltpu.VMEM((n_pp, 1, EX), F32),
            pltpu.VMEM((3, max(V, 2 * D8), TB), F32), pltpu.VMEM((4, D, TB), BF16),
            pltpu.VMEM((2, D8, TB), F32), pltpu.VMEM((1, TB), F32), pltpu.VMEM((1, TB), jnp.int32),
            pltpu.VMEM((n_pp, mb, seq), jnp.int32), pltpu.VMEM((4, CORES, 1, HALF), F32), pltpu.VMEM((4, 1, HALF), F32),
            pltpu.VMEM((4, nz, 1, HALF), F32), pltpu.VMEM((4, CORES, 1, HALF), F32),
            pltpu.VMEM((2, sum(HOPS), D8, LANE), F32), pltpu.VMEM((3, 2, D8, LANE), F32),
            pltpu.VMEM((2, D8, LANE), F32),
            dma((nsb, 2, HOPS[0])), dma((nsb, 2, HOPS[0])), dma((nsb, nz)), dma((nsb, nz)),
            dma((nsb, nz)), dma((2, 2)), dma((2, 2)), dma((2, sum(HOPS), 2)), dma((2, 2)),
            dma((4, nz + 1)), dma((4, nz + 1)), dma((n_pp - 1,)), dma((n_pp - 1,)), dma((4, TILES)), dma((3, 2)), dma((1,)),
            dma((sum(HOPS), PIECES)), dma((sum(HOPS), PIECES)), dma((2, sum(HOPS) + 1)),
            dma((n_pp - 1,)), dma((n_pp - 1,)),
            *[dma((2, HOPS[0] + 1, PIECES))] * 4,
        ],
        compiler_params=pltpu.CompilerParams(vmem_limit_bytes=63 * 1024 * 1024, collective_id=cid, has_side_effects=True),
        cost_estimate=pl.CostEstimate(flops=6 * n_pp * T * D * V, bytes_accessed=n_pp * T * D * 20, transcendentals=0),
        name="head")(hid, lab_own, gamma, WT)
    return out[:4]


def solution(mesh):
    n_pp = mesh.shape["pp"]

    def local_fn(hidden, labels, gamma, table):
        mb, seq, D = hidden.shape
        V = table.shape[0]
        T = mb * seq
        total = T * n_pp
        dh, dW, loss, sums = mega_call(jnp.swapaxes(hidden, 1, 2), labels, gamma.reshape(1, D), table.T,
                                       n_pp=n_pp, total=total)
        return (loss, jnp.swapaxes(dh, 1, 2), jnp.sum(sums[0, -LANE:])[None] / total, dW.T, sums[0, :D])

    token_spec = P(("dp", "pp"))
    return jax.shard_map(local_fn, mesh=mesh,
                         in_specs=(token_spec, token_spec, P(), P("pp")),
                         out_specs=(token_spec, token_spec, P("dp"), token_spec, P("dp")),
                         check_vma=False)
```

time: 444 us -> 419 us (0.944)
  other arithmetic: 13.5 us -> 1.23 us
  Pallas kernels: 408 us -> 402 us
  local copies, waits for them, and re-layouts: 18.6 us -> 13 us
    pallas_call x1 -> x0, Pallas kernels: 13.9 us -> none  [small_sum(): pl.pallas_call(functools.partial(sum_kernel, n_pp), out_shape=jax.ShapeDt...]
    pallas_call x1, Pallas kernels: 394 us -> 402 us  [mega_call(): pl.pallas_call(functools.partial(kernel, n_pp, float(total)), out_shape=[...]
    unnamed x24 -> x3, local copies, waits for them, and re-layouts: 13.5 us -> 10.4 us
where the time goes in v3:
time: 419 us; the launch traced here: 418 us
  Pallas kernels  402 us (96%)
  local copies, waits for them, and re-layouts  13 us (3%)
    pallas_call x1, Pallas kernels, mega_call(): pl.pallas_call(functools.partial(kernel, n_pp, float(total)), out_shape=[...  402 us
    unnamed x3, local copies, waits for them, and re-layouts  10.4 us

profile of v3, /device:TPU:21, one launch (start us, length us, event | category | flops | bytes accessed | tf_op | source)
XLA Modules:
  0.0 418.3 jit_solution(14588525419691123441)
XLA Ops:
  0.6 1.3 reshape.15.gamma
  1.9 401.6 %head.1 = (bf16[2,576,512]{2,1,0:T(8,128)(2,1)}, f32[576,3072]{1,0:T(8,128)}, f32[2,512]{1,0:T(2,128)}, f32[1,768]{1,0:T(1,128)}, bf16[16,576,1024]{2,1,0:T(8,12...) custom-call(bf16[2,576,512]{2,1,0:T(8,128)(2,1)} %bitcast.8, s32[2,512]{1,0:T(2,128)} %lab_own.1, ...), custom_call_target="tpu_custom_call" | custom-call | flops 173946175488 | bytes 188743680 | tf_op jit(solution)/shard_map/head/pallas_call | solution.py:544
  403.5 1.2 slice_reduce_fusion.1
  405.4 1.3 slice_reduce_fusion
  406.7 1.3 copy.12
  408.0 2.4 copy.13
  410.3 6.8 %copy.14 = f32[3072,576]{0,1:T(8,128)} copy(f32[3072,576]{0,1:T(8,128)} %bitcast.5) | data formatting | bytes 14155776

commit v4 on v3

--- a/solution.py
+++ b/solution.py
@@ -21,13 +21,14 @@
 PAD_ROWS = 8
 PIECES = 4
 WROWS = 256
+FWD_PARTS = 24
 HOPS = (4, 3)
 
 
 def kernel(n_pp, total, hid, lab_own, gamma, WT,
-           dh, dW, loss_out, ex_out, n_all, dnp, prx,
+           dh, dW_out, loss_out, ex_out, n_all, dnp, prx,
            n_own, W, gain, rinv, dgacc, lacc, s_out, ex_own, ex_rx,
-           U, nblk, dnb, svec, labm, lab_all, own_s, x1, x2, Sb, rx, ownv, sendb,
+           U, nblk, dW, dnb, svec, labm, tls, lab_all, own_s, x1, x2, Sb, rx, ownv, sendb,
            ag_recv, ag_send, pag_recv, pag_send, pair_recv, pair_send, dnp_sem, ring_recv, ring_send,
            st_recv, st_send, lab_recv, lab_send, nl_sem, ov_sem, io_sem, tail_recv, tail_send, tl_sem, ex_recv, ex_send,
            first_recv, first_send, firstp_recv, firstp_send):
@@ -82,19 +83,18 @@
 
     rows0 = D // PIECES
 
+    def first_tile(chip, p):
+        i = dev(chip)
+        return nblk.at[i // TILES, pl.ds(p * rows0, rows0), pl.ds(pl.multiple_of(lax.rem(i, TILES) * LANE, LANE), LANE)]
+
     def first_ring(d, r, p):
         g = sign(0, d)
-        rows = pl.ds(p * rows0, rows0)
-        src = n_own.at[rows, pl.ds(0, LANE)] if r == 0 else n_all.at[dev(z - g * r), rows, pl.ds(0, LANE)]
-        return remote(src, n_all.at[dev(z - g * r), rows, pl.ds(0, LANE)], first_send.at[d, r, p],
-                      first_recv.at[d, r, p], at(dev(z + g)))
+        ref = first_tile(z - g * r, p)
+        return remote(ref, ref, first_send.at[d, r, p], first_recv.at[d, r, p], at(dev(z + g)))
 
     def first_partner(d, r, p):
-        g = sign(0, d)
-        rows = pl.ds(p * rows0, rows0)
-        src = n_own.at[rows, pl.ds(0, LANE)] if r == 0 else n_all.at[dev(z - g * r), rows, pl.ds(0, LANE)]
-        return remote(src, n_all.at[dev(z - g * r), rows, pl.ds(0, LANE)], firstp_send.at[d, r, p],
-                      firstp_recv.at[d, r, p], partner)
+        ref = first_tile(z - sign(0, d) * r, p)
+        return remote(ref, ref, firstp_send.at[d, r, p], firstp_recv.at[d, r, p], partner)
 
     FIRSTP = [(d, r) for r in range(HOPS[0] + 1) for d in (0, 1) if r <= HOPS[d] and (r, d) != (0, 1)]
 
@@ -135,6 +135,10 @@
                                pair_recv.at[sb, chip], partner)))
         return out
 
+    def prx_arrived(sb, i):
+        remote(dnb.at[0, :, pl.ds(0, LANE)], prx.at[sb, i], pair_send.at[0, 0], pair_recv.at[sb, i],
+               partner).wait_recv()
+
     def tile_loads(sb, chip, k):
         chip = lax.rem(chip + 2 * nz, nz)
         return [pltpu.make_async_copy(dnp.at[sb, chip], ownv.at[k, 0], ov_sem.at[k, 0]),
@@ -219,6 +223,8 @@
 
     gain[...] = jnp.broadcast_to(1.0 + gamma[...], (LANE, D)).T
     norm_tile(0)
+    for p in range(PIECES):
+        first_tile(z, p)[...] = n_own[p * rows0:(p + 1) * rows0, 0:LANE]
     barrier = pltpu.get_barrier_semaphore()
     for k in range(1, n_pp):
         pl.semaphore_signal(barrier, inc=1, device_id=at(lax.rem(me + k, n_pp)), device_id_type=MESH)
@@ -255,47 +261,60 @@
                     first_partner(d, r, p).start()
         if r == HOPS[0] - 1 and nsb > 1:
             ag_first(1)
+    if nsb > 2:
+        ag_first(2)
     own_copy.wait()
     for d, r in FIRSTP:
         for p in range(PIECES):
             first_partner(d, r, p).wait_recv()
-    for c in n_loads(0):
-        c.start()
+    for k in range(1, n_pp):
+        lab_copy(k).wait_recv()
 
     base = me * V
 
     def forward(b):
-        for c in n_loads(b):
-            c.wait()
-        zl = jnp.dot(W[...], nblk[lax.rem(b, 4)], preferred_element_type=F32)
-        t = jnp.tanh(zl * (1.0 / SOFT_CAP))
-        U[lax.rem(b, 3), pl.ds(0, V), :] = t
-        s = jnp.sum(jnp.exp2(t * EXP2_SCALE).reshape(V // 8, 8, TB), axis=0)
-        s = jnp.sum(s, axis=0, keepdims=True)
-        for h in range(CORES):
-            own_s[lax.rem(b, 4), h] = s[:, h * HALF:(h + 1) * HALF]
-        st_pair(b).start()
-
-    def backward(b):
-        sl4 = lax.rem(b, 4)
-        st_back(b).wait_recv()
+        @pl.when(b >= per_sb)
+        def _():
+            for c in n_loads(b):
+                c.wait()
+        sl3 = lax.rem(b, 3)
         sb, j = b // per_sb, lax.rem(b, per_sb)
-        for h in range(CORES):
-            s = Sb[sl4, h]
-            s_out[b, :, h * HALF:(h + 1) * HALF] = s
-            svec[:, h * HALF:(h + 1) * HALF] = 1.0 / (s * total)
         for a in range(TILES):
             rows = lab_all[j * TILES + a, :, mb_lanes(sb)]
             row = rows[0:1]
             for m in range(1, rows.shape[0]):
                 row = jnp.where(sb // per_mb == m, rows[m:m + 1], row)
-            labm[:, a * LANE:(a + 1) * LANE] = row - base
-        t = U[lax.rem(b, 3), pl.ds(0, V), :]
-        p = jnp.exp2(t * EXP2_SCALE) * svec[...]
-        hit = lax.broadcasted_iota(jnp.int32, (V, TB), 0) == labm[...]
-        tl = jnp.sum(jnp.where(hit, t, 0.0).reshape(V // 8, 8, TB), axis=0)
-        g = p - jnp.where(hit, 1.0 / total, 0.0)
-        dz = (g * (1.0 - t * t)).astype(BF16)
+            labm[sl3, :, a * LANE:(a + 1) * LANE] = row - base
+        s = jnp.zeros((8, TB), F32)
+        tl = jnp.zeros((8, TB), F32)
+        n = V // FWD_PARTS
+        for c in range(FWD_PARTS):
+            zl = jnp.dot(W[c * n:(c + 1) * n, :], nblk[lax.rem(b, 4)], preferred_element_type=F32)
+            t = jnp.tanh(zl * (1.0 / SOFT_CAP))
+            e = jnp.exp2(t * EXP2_SCALE)
+            U[sl3, c * n:(c + 1) * n, :] = e * (1.0 - t * t)
+            hit = lax.broadcasted_iota(jnp.int32, (n, TB), 0) == labm[sl3] - c * n
+            s = s + jnp.sum(e.reshape(n // 8, 8, TB), axis=0)
+            tl = tl + jnp.sum(jnp.where(hit, t, 0.0).reshape(n // 8, 8, TB), axis=0)
+        tls[sl3] = tl
+        s = jnp.sum(s, axis=0, keepdims=True)
+        for h in range(CORES):
+            own_s[lax.rem(b, 4), h] = s[:, h * HALF:(h + 1) * HALF]
+        st_pair(b).start()
+
+    def backward(b):
+        sl4 = lax.rem(b, 4)
+        st_back(b).wait_recv()
+        sl3 = lax.rem(b, 3)
+        for h in range(CORES):
+            s = Sb[sl4, h]
+            s_out[b, :, h * HALF:(h + 1) * HALF] = s
+            svec[:, h * HALF:(h + 1) * HALF] = 1.0 / (s * total)
+        tl = tls[sl3]
+        t1 = jnp.sum(tl, axis=0, keepdims=True)
+        at_label = (1.0 - t1 * t1) * (1.0 / total)
+        hit = lax.broadcasted_iota(jnp.int32, (V, TB), 0) == labm[sl3]
+        dz = (U[sl3, pl.ds(0, V), :] * svec[...] - jnp.where(hit, at_label, 0.0)).astype(BF16)
         sl = lax.rem(b, 2)
         dnb[sl, pl.ds(0, D), :] = jnp.dot(WT[...], dz, preferred_element_type=F32)
         dnb[sl, pl.ds(D, PAD_ROWS), :] = tl
@@ -326,10 +345,22 @@
                 loss_out[m:m + 1, mb_lanes(sb)] = loss
         lacc[...] += loss
 
-    RS0 = per_sb + 3
+    RS0 = per_sb + 2
     n_rs = nsb - 1
 
+    def first_sent():
+        for p in range(PIECES):
+            for d in (0, 1):
+                for r in range(HOPS[d]):
+                    first_ring(d, r, p).wait_send()
+            for d, r in FIRSTP:
+                first_partner(d, r, p).wait_send()
+
     def step(s, _):
+        @pl.when(s == 2)
+        def _():
+            first_sent()
+
         @pl.when((s >= 1) & (s - 1 < nb))
         def _():
             b = s - 1
@@ -338,6 +369,8 @@
             x2[sl, z] = own_s[sl, core] + x1[sl]
             for k in range(1, nz):
                 st_chip(b, k).start()
+
+        ring_step(s - 1 - RS0, 1)
 
         @pl.when((s >= 2) & (s - 2 < nb))
         def _():
@@ -351,12 +384,17 @@
             Sb[sl, core] = acc
             st_back(b).start()
 
+        if nsb > 1:
+            for r in range(HOPS[0], 0, -1):
+                @pl.when(s == r - 1)
+                def _():
+                    ag_next(1, r)
         for r in range(HOPS[0], -1, -1):
-            u = s - r
-            sb = jnp.where(u <= 1, u + 2, jnp.where(u <= 5, u + 1, 7 + (u - 12) // 4))
-            now = ((u >= -1) & (u <= 1)) | ((u >= 3) & (u <= 5)) | ((u >= 12) & (lax.rem(u, 4) == 0))
-
-            @pl.when(now & (sb >= 1) & (sb < nsb))
+            u = s - 2 * r
+            sb = jnp.where(u <= 3, (u + 5) // 2, 5 + (u - 6) // 5)
+            now = ((u >= -1) & (u <= 3) & (lax.rem(u + 1, 2) == 0)) | ((u >= 6) & (lax.rem(u - 6, 5) == 0))
+
+            @pl.when(now & (sb < nsb))
             def _():
                 if r == 0:
                     ag_first(sb)
@@ -367,12 +405,12 @@
         def _():
             ag_wait((s + 1) // per_sb)
 
-        @pl.when(s + 1 < nb)
+        @pl.when((s + 1 >= per_sb) & (s + 1 < nb))
         def _():
             for c in n_loads(s + 1):
                 c.start()
 
-        @pl.when((s >= 4) & (s - 4 < nb))
+        @pl.when((s >= 4) & (s - 4 < nb) & (lax.rem(s, per_sb) != per_sb - 1))
         def _():
             for keep, give in dn_moves(s - 4):
                 keep.wait()
@@ -381,22 +419,17 @@
         q = s - RS0
         rsb, r = q // per_sb, lax.rem(q, per_sb)
 
-        @pl.when((q >= 0) & (rsb < n_rs) & (r == 0))
-        def _():
-            def body(i, _):
-                remote(dnb.at[0, :, pl.ds(0, LANE)], prx.at[rsb, i], pair_send.at[0, 0], pair_recv.at[rsb, i],
-                       partner).wait_recv()
-                return 0
-            lax.fori_loop(0, nz, body, 0)
-
-        @pl.when((q >= 0) & (rsb < n_rs))
-        def _():
+        def ring_loads():
             for d in (0, 1):
                 @pl.when(r < HOPS[d])
                 def _():
                     for c in tile_loads(rsb, ring_target(rsb, d, r), d):
                         c.start()
 
+        @pl.when((q >= 0) & (rsb < n_rs) & (r > 0))
+        def _():
+            ring_loads()
+
         last = (q >= per_sb) & (r == 0) & (rsb <= n_rs)
 
         @pl.when(last)
@@ -408,18 +441,23 @@
         def _():
             forward(s)
 
+        @pl.when((q >= 0) & (rsb < n_rs) & (r == 0))
+        def _():
+            for keep, give in dn_moves(s - 3):
+                keep.wait()
+                give.wait_send()
+
+            def body(i, _):
+                prx_arrived(rsb, i)
+                return 0
+            lax.fori_loop(0, nz, body, 0)
+            ring_loads()
+
         ring_step(q, 0)
 
-        @pl.when(s == 2)
-        def _():
-            for k in range(1, n_pp):
-                lab_copy(k).wait_recv()
-
         @pl.when((s >= 2) & (s - 2 < nb))
         def _():
             backward(s - 2)
-
-        ring_step(q, 1)
 
         @pl.when(last)
         def _():
@@ -430,14 +468,17 @@
 
     sb = nsb - 1
     par = sb % 2
-    for b in range(max(n_steps - 4, 0), nb):
+    assert n_steps == nb + 2
+    w_store = pltpu.make_async_copy(dW, dW_out, io_sem.at[0])
+    w_store.start()
+    ring_step(jnp.int32(n_steps - 1 - RS0), 1)
+    for b in range(nb - 2, nb):
         for keep, give in dn_moves(b):
             keep.wait()
             give.wait_send()
 
     def prx_wait(i, _):
-        remote(dnb.at[0, :, pl.ds(0, LANE)], prx.at[sb, i], pair_send.at[0, 0], pair_recv.at[sb, i],
-               partner).wait_recv()
+        prx_arrived(sb, i)
         return 0
     lax.fori_loop(0, nz, prx_wait, 0)
 
@@ -469,7 +510,25 @@
     if n_rs > 0:
         for c in tile_loads(n_rs - 1, z, 2):
             c.start()
+    def old_sends():
+        for k in range(1, n_pp):
+            lab_copy(k).wait_send()
+
+        def finish(sb, _):
+            for d in (0, 1):
+                for r in range(HOPS[d]):
+                    ag_ring(sb, d, r).wait_send()
+
+            def body(i, _):
+                ag_partner(sb, i).wait_send()
+                return 0
+            lax.fori_loop(0, nz, body, 0)
+            return 0
+        lax.fori_loop(1, nsb, finish, 0)
+
     for e, (d, r) in enumerate(hops):
+        if r == 1 and d == 0:
+            old_sends()
         if r == 1 and d == 0 and n_rs > 0:
             for h in (0, 1):
                 ring_step(jnp.int32(n_rs * per_sb), h)
@@ -509,27 +568,7 @@
     for e in range(len(hops)):
         for p in range(PIECES):
             tail_copy(e, p).wait_send()
-    for k in range(1, n_pp):
-        lab_copy(k).wait_send()
-
-    for p in range(PIECES):
-        for d in (0, 1):
-            for r in range(HOPS[d]):
-                first_ring(d, r, p).wait_send()
-        for d, r in FIRSTP:
-            first_partner(d, r, p).wait_send()
-
-    def finish(sb, _):
-        for d in (0, 1):
-            for r in range(HOPS[d]):
-                ag_ring(sb, d, r).wait_send()
-
-        def body(i, _):
-            ag_partner(sb, i).wait_send()
-            return 0
-        lax.fori_loop(0, nz, body, 0)
-        return 0
-    lax.fori_loop(1, nsb, finish, 0)
+    w_store.wait()
 
 
 def mega_call(hid, lab_own, gamma, WT, *, n_pp, total, cid=1):
@@ -546,13 +585,14 @@
         out_shape=[sd((mb, D, seq), BF16), sd((D, V), F32), sd((mb, seq), F32), sd((1, EX), F32),
                    sd((n_pp, D, T), BF16), sd((nsb, nz, D8, LANE), F32), sd((nsb, nz, D8, LANE), F32)],
         in_specs=[vmem] * 4,
-        out_specs=[vmem, vmem, vmem, vmem, hbm, hbm, hbm],
+        out_specs=[vmem, hbm, vmem, vmem, hbm, hbm, hbm],
         scratch_shapes=[
             pltpu.VMEM((D, T), BF16), pltpu.VMEM((V, D), BF16), pltpu.VMEM((D, LANE), F32), pltpu.VMEM((nsb, 1, LANE), F32),
             pltpu.VMEM((D, LANE), F32), pltpu.VMEM((1, LANE), F32), pltpu.VMEM((nb, 1, TB), F32),
             pltpu.VMEM((1, EX), F32), pltpu.VMEM((n_pp, 1, EX), F32),
-            pltpu.VMEM((3, max(V, 2 * D8), TB), F32), pltpu.VMEM((4, D, TB), BF16),
-            pltpu.VMEM((2, D8, TB), F32), pltpu.VMEM((1, TB), F32), pltpu.VMEM((1, TB), jnp.int32),
+            pltpu.VMEM((3, max(V, 2 * D8), TB), F32), pltpu.VMEM((4, D, TB), BF16), pltpu.VMEM((D, V), F32),
+            pltpu.VMEM((2, D8, TB), F32), pltpu.VMEM((1, TB), F32), pltpu.VMEM((3, 1, TB), jnp.int32),
+            pltpu.VMEM((3, 8, TB), F32),
             pltpu.VMEM((n_pp, mb, seq), jnp.int32), pltpu.VMEM((4, CORES, 1, HALF), F32), pltpu.VMEM((4, 1, HALF), F32),
             pltpu.VMEM((4, nz, 1, HALF), F32), pltpu.VMEM((4, CORES, 1, HALF), F32),
             pltpu.VMEM((2, sum(HOPS), D8, LANE), F32), pltpu.VMEM((3, 2, D8, LANE), F32),

time: 419 us -> 377 us (0.90)
  Pallas kernels: 402 us -> 360 us
    pallas_call x1, Pallas kernels: 402 us -> 360 us  [mega_call(): pl.pallas_call(functools.partial(kernel, n_pp, float(total)), out_shape=[...]
where the time goes in v4:
time: 377 us
  Pallas kernels  360 us (95%)
  local copies, waits for them, and re-layouts  13 us (3%)
    pallas_call x1, Pallas kernels, mega_call(): pl.pallas_call(functools.partial(kernel, n_pp, float(total)), out_shape=[...  360 us
    unnamed x3, local copies, waits for them, and re-layouts  10.4 us

profile of v4, /device:TPU:21, one launch (start us, length us, event | category | flops | bytes accessed | tf_op | source)
XLA Modules:
  0.0 376.8 jit_solution(14664209069261241223)
XLA Ops:
  0.6 1.3 reshape.15.gamma
  1.9 360.1 %head.1 = (bf16[2,576,512]{2,1,0:T(8,128)(2,1)}, f32[576,3072]{1,0:T(8,128)}, f32[2,512]{1,0:T(2,128)}, f32[1,768]{1,0:T(1,128)}, bf16[16,576,1024]{2,1,0:T(8,12...) custom-call(bf16[2,576,512]{2,1,0:T(8,128)(2,1)} %bitcast.8, s32[2,512]{1,0:T(2,128)} %lab_own.1, ...), custom_call_target="tpu_custom_call" | custom-call | flops 173946175488 | bytes 188743680 | tf_op jit(solution)/shard_map/head/pallas_call | solution.py:583
  362.0 1.2 slice_reduce_fusion.1
  363.9 1.3 slice_reduce_fusion
  365.2 1.3 copy.12
  366.5 2.4 copy.13
  368.8 6.8 %copy.14 = f32[3072,576]{0,1:T(8,128)} copy(f32[3072,576]{0,1:T(8,128)} %bitcast.5) | data formatting | bytes 14155776

commit v5 on v4

--- a/solution.py
+++ b/solution.py
@@ -20,6 +20,7 @@
 HALF = TB // CORES
 PAD_ROWS = 8
 PIECES = 4
+TAIL_PIECES = 6
 WROWS = 256
 FWD_PARTS = 24
 HOPS = (4, 3)
@@ -221,13 +222,13 @@
         rows = pl.ds(pl.multiple_of(c * wrows, wrows), wrows)
         W[rows, :] = WT[:, rows].T
 
+    barrier = pltpu.get_barrier_semaphore()
+    for k in range(1, n_pp):
+        pl.semaphore_signal(barrier, inc=1, device_id=at(lax.rem(me + k, n_pp)), device_id_type=MESH)
     gain[...] = jnp.broadcast_to(1.0 + gamma[...], (LANE, D)).T
     norm_tile(0)
     for p in range(PIECES):
         first_tile(z, p)[...] = n_own[p * rows0:(p + 1) * rows0, 0:LANE]
-    barrier = pltpu.get_barrier_semaphore()
-    for k in range(1, n_pp):
-        pl.semaphore_signal(barrier, inc=1, device_id=at(lax.rem(me + k, n_pp)), device_id_type=MESH)
     pl.semaphore_wait(barrier, n_pp - 1)
     for p in range(PIECES):
         for d in (0, 1):
@@ -318,10 +319,10 @@
         sl = lax.rem(b, 2)
         dnb[sl, pl.ds(0, D), :] = jnp.dot(WT[...], dz, preferred_element_type=F32)
         dnb[sl, pl.ds(D, PAD_ROWS), :] = tl
-        dW[...] += lax.dot_general(nblk[sl4], dz, (((1,), (1,)), ((), ())), preferred_element_type=F32)
         for keep, give in dn_moves(b):
             keep.start()
             give.start()
+        dW[...] += lax.dot_general(nblk[sl4], dz, (((1,), (1,)), ((), ())), preferred_element_type=F32)
         st_pair(b).wait_send()
         for k in range(1, nz):
             st_chip(b, k).wait_send()
@@ -385,14 +386,13 @@
             st_back(b).start()
 
         if nsb > 1:
-            for r in range(HOPS[0], 0, -1):
-                @pl.when(s == r - 1)
-                def _():
-                    ag_next(1, r)
+            @pl.when(s == HOPS[0] - 1)
+            def _():
+                ag_next(1, HOPS[0])
         for r in range(HOPS[0], -1, -1):
             u = s - 2 * r
-            sb = jnp.where(u <= 3, (u + 5) // 2, 5 + (u - 6) // 5)
-            now = ((u >= -1) & (u <= 3) & (lax.rem(u + 1, 2) == 0)) | ((u >= 6) & (lax.rem(u - 6, 5) == 0))
+            sb = jnp.where(u <= 0, u + 3, jnp.where(u <= 4, u + 1, 6 + (u - 9) // 5))
+            now = ((u >= -1) & (u <= 0)) | ((u >= 3) & (u <= 4)) | ((u >= 9) & (lax.rem(u - 9, 5) == 0))
 
             @pl.when(now & (sb < nsb))
             def _():
@@ -437,10 +437,6 @@
             for c in tile_loads(rsb - 1, z, 2):
                 c.start()
 
-        @pl.when(s < nb)
-        def _():
-            forward(s)
-
         @pl.when((q >= 0) & (rsb < n_rs) & (r == 0))
         def _():
             for keep, give in dn_moves(s - 3):
@@ -453,7 +449,17 @@
             lax.fori_loop(0, nz, body, 0)
             ring_loads()
 
+        @pl.when(s < nb)
+        def _():
+            forward(s)
+
         ring_step(q, 0)
+
+        if nsb > 1:
+            for r in range(HOPS[0] - 1, 0, -1):
+                @pl.when(s == r - 1)
+                def _():
+                    ag_next(1, r)
 
         @pl.when((s >= 2) & (s - 2 < nb))
         def _():
@@ -493,7 +499,7 @@
                       pltpu.make_async_copy(prx.at[sb, chip], slot(1, e), tl_sem.at[1, e])])
         for c in loads[-1]:
             c.start()
-    cuts = [D8 // 8 * p // PIECES * 8 for p in range(PIECES + 1)]
+    cuts = [D8 // 8 * p // TAIL_PIECES * 8 for p in range(TAIL_PIECES + 1)]
 
     def piece(p):
         return pl.ds(cuts[p], cuts[p + 1] - cuts[p])
@@ -535,7 +541,7 @@
             own_tile(n_rs - 1)
         for c in loads[e]:
             c.wait()
-        for p in range(PIECES):
+        for p in range(TAIL_PIECES):
             mine, other = slot(0, e).at[piece(p)], slot(1, e).at[piece(p)]
             if r > 0:
                 tail_arrived(d, r - 1, p)
@@ -546,7 +552,7 @@
     for c in loads[len(hops)]:
         c.wait()
     for d in (0, 1):
-        for p in range(PIECES):
+        for p in range(TAIL_PIECES):
             tail_arrived(d, HOPS[d] - 1, p)
     finish_tile(sb, slot(0, len(hops))[...] + slot(1, len(hops))[...] + rx[par, HOPS[0] - 1]
                 + rx[par, HOPS[0] + HOPS[1] - 1])
@@ -566,7 +572,7 @@
     for c in exs:
         c.wait_send()
     for e in range(len(hops)):
-        for p in range(PIECES):
+        for p in range(TAIL_PIECES):
             tail_copy(e, p).wait_send()
     w_store.wait()
 
@@ -600,7 +606,7 @@
             dma((nsb, 2, HOPS[0])), dma((nsb, 2, HOPS[0])), dma((nsb, nz)), dma((nsb, nz)),
             dma((nsb, nz)), dma((2, 2)), dma((2, 2)), dma((2, sum(HOPS), 2)), dma((2, 2)),
             dma((4, nz + 1)), dma((4, nz + 1)), dma((n_pp - 1,)), dma((n_pp - 1,)), dma((4, TILES)), dma((3, 2)), dma((1,)),
-            dma((sum(HOPS), PIECES)), dma((sum(HOPS), PIECES)), dma((2, sum(HOPS) + 1)),
+            dma((sum(HOPS), TAIL_PIECES)), dma((sum(HOPS), TAIL_PIECES)), dma((2, sum(HOPS) + 1)),
             dma((n_pp - 1,)), dma((n_pp - 1,)),
             *[dma((2, HOPS[0] + 1, PIECES))] * 4,
         ],
@@ -610,6 +616,32 @@
     return out[:4]
 
 
+def copy_kernel(parts, a, b, oa, ob, va, vb, sa, sb):
+    rows = a.shape[0] // parts
+    cut = [pl.ds(i * rows, rows) for i in range(parts)]
+    into = [pltpu.make_async_copy(a.at[c], va.at[c], sa.at[0, i]) for i, c in enumerate(cut)]
+    away = [pltpu.make_async_copy(va.at[c], oa.at[c], sa.at[1, i]) for i, c in enumerate(cut)]
+    into.append(pltpu.make_async_copy(b, vb, sb.at[0]))
+    away.append(pltpu.make_async_copy(vb, ob, sb.at[1]))
+    for c in into:
+        c.start()
+    for c, d in zip(into, away):
+        c.wait()
+        d.start()
+    for d in away:
+        d.wait()
+
+
+def own_buffers(a, b, parts=12):
+    hbm = pl.BlockSpec(memory_space=pl.ANY)
+    sd, dma = jax.ShapeDtypeStruct, pltpu.SemaphoreType.DMA
+    return pl.pallas_call(
+        functools.partial(copy_kernel, parts), out_shape=[sd(a.shape, a.dtype), sd(b.shape, b.dtype)],
+        in_specs=[hbm] * 2, out_specs=[hbm] * 2,
+        scratch_shapes=[pltpu.VMEM(a.shape, a.dtype), pltpu.VMEM(b.shape, b.dtype), dma((2, parts)), dma((2,))],
+        compiler_params=pltpu.CompilerParams(vmem_limit_bytes=56 * 1024 * 1024), name="own_buffers")(a, b)
+
+
 def solution(mesh):
     n_pp = mesh.shape["pp"]
 
@@ -620,6 +652,7 @@
         total = T * n_pp
         dh, dW, loss, sums = mega_call(jnp.swapaxes(hidden, 1, 2), labels, gamma.reshape(1, D), table.T,
                                        n_pp=n_pp, total=total)
+        dW, dh = own_buffers(dW, dh)
         return (loss, jnp.swapaxes(dh, 1, 2), jnp.sum(sums[0, -LANE:])[None] / total, dW.T, sums[0, :D])
 
     token_spec = P(("dp", "pp"))

time: 377 us -> 371 us (0.984)
  local copies, waits for them, and re-layouts: 13 us -> 3.16 us
  Pallas kernels: 360 us -> 364 us
    unnamed x3, local copies, waits for them, and re-layouts: 10.4 us -> 0.6 us
    pallas_call x0 -> x1, Pallas kernels: none -> 6.52 us  [own_buffers(): pl.pallas_call(functools.partial(copy_kernel, parts), out_shape=[sd(a.sha...]
where the time goes in v5:
time: 371 us
  Pallas kernels  364 us (98%)
    pallas_call x1, Pallas kernels, mega_call(): pl.pallas_call(functools.partial(kernel, n_pp, float(total)), out_shape=[...  358 us

profile of v5, /device:TPU:21, one launch (start us, length us, event | category | flops | bytes accessed | tf_op | source)
XLA Modules:
  0.0 371.2 jit_solution(13752917349631422971)
XLA Ops:
  0.6 1.3 reshape.15.gamma
  1.9 357.8 %head.1 = (bf16[2,576,512]{2,1,0:T(8,128)(2,1)}, f32[576,3072]{1,0:T(8,128)}, f32[2,512]{1,0:T(2,128)}, f32[1,768]{1,0:T(1,128)}, bf16[16,576,1024]{2,1,0:T(8,12...) custom-call(bf16[2,576,512]{2,1,0:T(8,128)(2,1)} %bitcast.7, s32[2,512]{1,0:T(2,128)} %lab_own.1, ...), custom_call_target="tpu_custom_call" | custom-call | flops 173946175488 | bytes 188743680 | tf_op jit(solution)/shard_map/head/pallas_call | solution.py:589
  359.7 0.0 copy-start
  359.7 1.2 slice_reduce_fusion.1
  361.6 1.3 slice_reduce_fusion
  362.9 6.5 %own_buffers.1 = (f32[576,3072]{1,0:T(8,128)}, bf16[2,576,512]{2,1,0:T(8,128)(2,1)}) custom-call(f32[576,3072]{1,0:T(8,128)} %get-tuple-element.12.a, bf16[2,576,512]{2,1,0:T(8,128)(2,1)} %get-tuple-element.13.b), custom_call_target="tpu_custom_call" | custom-call | tf_op jit(solution)/shard_map/own_buffers/pallas_call | solution.py:638
  369.4 0.0 copy-done
  369.5 0.6 copy.10
Async XLA Ops:
  359.7 9.7 %copy-start = (f32[2,512]{1,0:T(2,128)S(1)}, f32[2,512]{1,0:T(2,128)}, u32[]{:S(2)}) copy-start(f32[2,512]{1,0:T(2,128)} %get-tuple-element.22) | copy-start | bytes 12292
